TPU v7x, 512 devices: a whole 4x8x8 slice. The times are simulated.
512 devices in a mesh: dp: 64 (over z, x, core), rows: 8 (over y).
Axes of the slice: x: 4, y: 8, z: 8, core: 2. Of those that a mesh axis runs over, the one named last changes fastest.
Arguments:
- fine_level: bfloat16 [64, 128, 64, 256], P('dp', 'rows'), may hold values from -6 to 6
- out_grad: bfloat16 [64, 128, 64, 256], P('dp', 'rows'), may hold values from -6 to 6
- fine_input: bfloat16 [64, 128, 64, 256], P('dp', 'rows'), may hold values from -6 to 6
- mid_input: bfloat16 [64, 64, 32, 512], P('dp', None, None, 'rows'), may hold values from -6 to 6
- top_input: bfloat16 [64, 32, 16, 1024], P('dp', None, None, 'rows'), may hold values from -6 to 6
- smooth_weight: bfloat16 [3, 3, 256, 256], replicated, may hold values from -0.125 to 0.125
- fine_lateral: bfloat16 [256, 256], replicated, may hold values from -0.375 to 0.375
- mid_lateral: bfloat16 [512, 256], P('rows'), may hold values from -0.375 to 0.375
- top_lateral: bfloat16 [1024, 256], P('rows'), may hold values from -0.375 to 0.375
Outputs:
- grad_fine: bfloat16 [64, 128, 64, 256], P('dp', 'rows')
- grad_mid: bfloat16 [64, 64, 32, 512], P('dp', None, None, 'rows')
- grad_top: bfloat16 [64, 32, 16, 1024], P('dp', None, None, 'rows')
- kernel_grads: float32 [2560, 256], P('dp')
- midlat_grad: float32 [512, 256], P('rows')
- toplat_grad: float32 [1024, 256], P('rows')
All inputs are finite; a program needn't handle non-finite values.
Results may differ from a plain program's by a relative error of at most 0.0062.
Values may be sent and summed in bfloat16 or wider, within the bound.
A program may use at most 64 MiB of HBM per device.

v0:
```python
import jax
import jax.numpy as jnp
from jax import lax
from jax.sharding import Mesh
from jax.sharding import PartitionSpec as P

DP = ("dp_0", "dp_1", "dp_2")


def with_halo(value, sides, width):
    for axis, dim in sides:
        count, length = (lax.axis_size(axis), value.shape[dim])
        up = [(i, (i + 1) % count) for i in range(count - 1)]
        down = [(j, i) for i, j in up]
        last = lax.slice_in_dim(value, length - width, length, axis=dim)
        leading = lax.slice_in_dim(value, 0, width, axis=dim)
        before = lax.ppermute(last, axis, up)
        after = lax.ppermute(leading, axis, down)
        value = jnp.concatenate([before, value, after], axis=dim)
    return value


def cut_along(value, dim, count):
    before, after = (value.shape[:dim], value.shape[dim + 1 :])
    return jnp.moveaxis(value.reshape(*before, count, -1, *after), dim, 0)


def sum_at_owner(value, axis, dim):
    count = lax.axis_size(axis)
    blocks = lax.all_to_all(cut_along(value, dim, count), axis, 0, 0, tiled=True)
    return jnp.sum(blocks.astype(jnp.float32), axis=0)


def sum_by_axis(value, axes, dim):
    far, near = axes
    own = sum_at_owner(cut_along(value, dim, lax.axis_size(far)), near, dim + 1)
    return jnp.sum(
        lax.all_to_all(own.astype(jnp.bfloat16), far, 0, 0, tiled=True).astype(jnp.float32), axis=0
    )


def sent_to_all(value, axis):
    count = lax.axis_size(axis)
    return lax.all_to_all(
        jnp.broadcast_to(value[None], (count, *value.shape)), axis, 0, 0, tiled=True
    )


def over_copies(value, axis):
    return sent_to_all(value, axis).sum(axis=0)


def in_order(blocks, dim):
    shape = list(blocks.shape[1:])
    shape[dim] *= blocks.shape[0]
    return jnp.moveaxis(blocks, 0, dim).reshape(shape)


def gathered_copies(value, axis, dim):
    return in_order(sent_to_all(value, axis), dim)


def rows_for(lines, count):
    spare = -lines.shape[0] % count
    if not spare:
        return lines
    return jnp.concatenate([lines, jnp.zeros((spare, *lines.shape[1:]), lines.dtype)])


def sum_by_parts(value, axes):
    lines = value.reshape(-1, value.shape[-1])
    padded = rows_for(lines, lax.axis_size(axes))
    whole = gathered_copies(sum_at_owner(padded, axes, 0).astype(jnp.bfloat16), axes, 0)
    return lax.slice_in_dim(whole, 0, len(lines)).reshape(value.shape).astype(jnp.float32)


def pool_two(field):
    images, rows_n, cols_n, chans = field.shape
    return field.reshape(images, rows_n // 2, 2, cols_n // 2, 2, chans).sum(axis=(2, 4))


def contract_last(left, right):
    return lax.dot_general(
        left, right, (((1,), (1,)), ((), ())), preferred_element_type=jnp.float32
    )


def contract_first(left, right):
    return lax.dot_general(
        left, right, (((0,), (0,)), ((), ())), preferred_element_type=jnp.float32
    )


def body(
    fine_level,
    out_grad,
    fine_input,
    mid_input,
    top_input,
    smooth_weight,
    fine_lateral,
    mid_lateral,
    top_lateral,
):
    images, strip, width, chans = out_grad.shape
    cells = images * strip * width
    rimmed = with_halo(out_grad, (("rows", 1),), 1)
    rimmed = jnp.pad(rimmed, ((0, 0), (0, 0), (1, 1), (0, 0)))
    fine_flat = fine_level.reshape(cells, chans)
    level_grad = jnp.zeros((cells, chans), jnp.float32)
    pieces = []
    for tap_a in range(3):
        for tap_b in range(3):
            shifted = rimmed[
                :, 2 - tap_a : 2 - tap_a + strip, 2 - tap_b : 2 - tap_b + width, :
            ].reshape(cells, chans)
            level_grad = level_grad + contract_last(shifted, smooth_weight[tap_a, tap_b])
            pieces.append(contract_first(fine_flat, shifted))
    fine_grad = level_grad.astype(jnp.bfloat16)
    grad_fine = (
        contract_last(fine_grad, fine_lateral)
        .astype(jnp.bfloat16)
        .reshape(images, strip, width, -1)
    )
    pieces.append(contract_first(fine_input.reshape(cells, -1), fine_grad))
    kernel_term = jnp.concatenate(pieces, axis=0)
    share = sum_by_axis(kernel_term.astype(jnp.bfloat16), (("dp_0", "dp_1"), "dp_2"), 0)
    kernel_grads = over_copies(share, "rows")
    pooled = pool_two(level_grad.reshape(images, strip, width, chans)).astype(jnp.bfloat16)
    mid_grad = gathered_copies(pooled, "rows", 1)
    top_grad = pool_two(mid_grad.astype(jnp.float32)).astype(jnp.bfloat16)
    mid_flat = mid_grad.reshape(-1, chans)
    top_flat = top_grad.reshape(-1, chans)
    grad_mid = contract_last(mid_flat, mid_lateral).astype(jnp.bfloat16).reshape(mid_input.shape)
    grad_top = contract_last(top_flat, top_lateral).astype(jnp.bfloat16).reshape(top_input.shape)
    mid_term = contract_first(mid_input.reshape(mid_flat.shape[0], -1), mid_flat)
    top_term = contract_first(top_input.reshape(top_flat.shape[0], -1), top_flat)
    midlat_grad, toplat_grad = (
        sum_by_parts(mid_term.astype(jnp.bfloat16), DP),
        sum_by_parts(top_term.astype(jnp.bfloat16), DP),
    )
    return (grad_fine, grad_mid, grad_top, kernel_grads, midlat_grad, toplat_grad)


def solution(mesh):
    torus = Mesh(
        mesh.devices.reshape(8, 4, 2, mesh.shape["rows"]), ("dp_0", "dp_1", "dp_2", "rows")
    )
    return jax.shard_map(
        body,
        mesh=torus,
        in_specs=(
            P(DP, "rows", None, None),
            P(DP, "rows", None, None),
            P(DP, "rows", None, None),
            P(DP, None, None, "rows"),
            P(DP, None, None, "rows"),
            P(),
            P(),
            P("rows", None),
            P("rows", None),
        ),
        out_specs=(
            P(DP, "rows", None, None),
            P(DP, None, None, "rows"),
            P(DP, None, None, "rows"),
            P(DP, None),
            P("rows", None),
            P("rows", None),
        ),
        check_vma=False,
    )
```

profile of v0, /device:TPU:1, one launch (start us, length us, event | category | flops | bytes accessed | tf_op | source)
XLA Modules:
  0.0 176.3 jit_solution(4260781229022245208)
XLA Ops:
  0.6 0.8 fusion.86
  1.5 4.0 %collective-permute-start = (bf16[1,1,64,256]{3,2,1,0:T(8,128)(2,1)S(1)}, bf16[1,1,64,256]{3,2,1,0:T(8,128)(2,1)S(1)}, u32[]{:S(2)}, u32[]{:S(2)}) collective-permute-start(bf16[1,1,64,256]{3,2,1,0:T(8,128)(2,1)S(1)} %get-tuple-element.20), channel_id=1, source_target_pairs={{0,1},{1,2},{2,3},{3,4},{4,5},{5,6},{6,7},{8,9},{9,10},{10,11},{11... | collective-permute-start | bytes 98312 | tf_op jit(solution)/shard_map/ppermute | solution.py:17
  5.5 1.3 collective-permute-start.1
  6.8 3.3 %collective-permute-done.1 = bf16[1,1,64,256]{3,2,1,0:T(8,128)(2,1)S(1)} collective-permute-done((bf16[1,1,64,256]{3,2,1,0:T(8,128)(2,1)S(1)}, bf16[1,1,64,256]{3,2,1,0:T(8,128)(2,1)S(1)}, u32[]{:S(2)}, u32[]{:S(2)}) %collective-permute-start.1) | collective-permute-done | bytes 32800 | tf_op jit(solution)/shard_map/ppermute | solution.py:18
  10.2 1.3 fusion.37
  11.5 0.5 fusion.85
  12.0 0.7 copy-done.2
  13.4 0.4 fusion.27
  13.8 0.6 copy-done.1
  16.3 0.4 fusion.17
  19.8 0.7 copy-done.3
  20.9 9.7 %all_to_all.40 = bf16[2,32,40,256]{3,2,1,0:T(8,128)(2,1)S(1)} all-to-all(bf16[2,32,40,256]{3,2,1,0:T(8,128)(2,1)S(1)} %bitcast.239), channel_id=1, replica_groups=mesh['dp_0'=8,'dp_1'=4,'dp_2'=2,'rows'=8] {'dp_2'}, dimensions={0} | all-to-all | bytes 2621440 | tf_op jit(solution)/shard_map/all_to_all | solution.py:30
  30.6 1.2 reduce_sum.74
  31.9 9.7 %all-to-all-start.2 = ((bf16[32,40,256]{2,1,0:T(8,128)(2,1)}), bf16[32,40,256]{2,1,0:T(8,128)(2,1)S(1)}, u32[]{:S(2)}, u32[]{:S(2)}) async-start(bf16[32,40,256]{2,1,0:T(8,128)(2,1)} %reduce_sum.74), calls=%async_computation.2 | async-start | bytes 1310720 | tf_op jit(solution)/shard_map/all_to_all | solution.py:38
  41.6 0.6 reshape_reshape.4
  42.2 0.9 reduce_sum.72
  43.1 17.3 %all-to-all-done.2 = bf16[32,40,256]{2,1,0:T(8,128)(2,1)S(1)} async-done(((bf16[32,40,256]{2,1,0:T(8,128)(2,1)}), bf16[32,40,256]{2,1,0:T(8,128)(2,1)S(1)}, u32[]{:S(2)}, u32[]{:S(2)}) %all-to-all-start.2) | async-done | bytes 655392 | tf_op jit(solution)/shard_map/all_to_all | solution.py:38
  60.4 1.1 broadcast_in_dim.8
  61.5 7.0 %all-to-all-start = ((bf16[8,1,8,32,256]{4,3,2,1,0:T(8,128)(2,1)}), bf16[8,1,8,32,256]{4,3,2,1,0:T(8,128)(2,1)S(1)}, u32[]{:S(2)}, u32[]{:S(2)}) async-start(bf16[8,1,8,32,256]{4,3,2,1,0:T(8,128)(2,1)} %broadcast_in_dim.8), calls=%async_computation | async-start | bytes 2097152 | tf_op jit(solution)/shard_map/all_to_all | solution.py:44
  68.6 27.2 %all-to-all-done = bf16[8,1,8,32,256]{4,3,2,1,0:T(8,128)(2,1)S(1)} async-done(((bf16[8,1,8,32,256]{4,3,2,1,0:T(8,128)(2,1)}), bf16[8,1,8,32,256]{4,3,2,1,0:T(8,128)(2,1)S(1)}, u32[]{:S(2)}, u32[]{:S(2)}) %all-to-all-start) | async-done | bytes 1048608 | tf_op jit(solution)/shard_map/all_to_all | solution.py:44
  95.8 0.7 broadcast_in_dim.9
  96.6 3.4 %all-to-all-start.3 = ((f32[8,40,256]{2,1,0:T(8,128)}), f32[8,40,256]{2,1,0:T(8,128)S(1)}, u32[]{:S(2)}, u32[]{:S(2)}) async-start(f32[8,40,256]{2,1,0:T(8,128)} %broadcast_in_dim.9), calls=%async_computation.3 | async-start | bytes 655360 | tf_op jit(solution)/shard_map/all_to_all | solution.py:44
  100.0 1.3 fusion.32
  101.3 0.5 broadcast.20
  101.9 0.7 reduce.8
  102.5 0.6 reshape.193
  103.2 1.2 convert_element_type.92
  104.4 3.0 %reduce.7 = bf16[32,16,256]{2,1,0:T(8,128)(2,1)S(1)} reduce(bf16[32,2,16,2,256]{4,3,2,1,0:T(2,128)(2,1)} %convert_element_type.92, bf16[]{:T(256)} %constant.6.clone.1), dimensions={1,3}, to_apply=%region_1.2.clone | reduce | flops 393216 | bytes 1310722 | tf_op jit(solution)/shard_map/reduce_sum | solution.py:79
  107.3 2.6 %all-to-all-done.3 = f32[8,40,256]{2,1,0:T(8,128)S(1)} async-done(((f32[8,40,256]{2,1,0:T(8,128)}), f32[8,40,256]{2,1,0:T(8,128)S(1)}, u32[]{:S(2)}, u32[]{:S(2)}) %all-to-all-start.3) | async-done | bytes 327712 | tf_op jit(solution)/shard_map/all_to_all | solution.py:44
  109.9 12.2 %all-to-all-start.4 = ((bf16[64,2,128]{2,1,0:T(2,128)(2,1)}), bf16[64,2,128]{2,1,0:T(2,128)(2,1)S(1)}, u32[]{:S(2)}, u32[]{:S(2)}) async-start(bf16[64,2,128]{2,1,0:T(2,128)(2,1)} %reshape.193), calls=%async_computation.4 | async-start | bytes 65536 | tf_op jit(solution)/shard_map/all_to_all | solution.py:30
  122.3 0.7 reshape.180
  123.0 8.4 %all-to-all-done.4 = bf16[64,2,128]{2,1,0:T(2,128)(2,1)S(1)} async-done(((bf16[64,2,128]{2,1,0:T(2,128)(2,1)}), bf16[64,2,128]{2,1,0:T(2,128)(2,1)S(1)}, u32[]{:S(2)}, u32[]{:S(2)}) %all-to-all-start.4) | async-done | bytes 32800 | tf_op jit(solution)/shard_map/all_to_all | solution.py:30
  131.4 4.7 %all-to-all-start.6 = ((bf16[64,2,256]{2,1,0:T(2,128)(2,1)}), bf16[64,2,256]{2,1,0:T(2,128)(2,1)S(1)}, u32[]{:S(2)}, u32[]{:S(2)}) async-start(bf16[64,2,256]{2,1,0:T(2,128)(2,1)} %reshape.180), calls=%async_computation.6 | async-start | bytes 131072 | tf_op jit(solution)/shard_map/all_to_all | solution.py:30
  136.2 2.0 %convolution_convert_fusion.1 = bf16[1024,256]{1,0:T(8,128)(2,1)} fusion(bf16[256,256]{1,0:T(8,128)(2,1)} %param.15, f32[1024,256]{1,0:T(8,128)S(1)} %fusion), kind=kOutput, calls=%fused_computation.14 | convolution fusion | flops 134742016 | bytes 1703936 | tf_op jit(solution)/shard_map/dot_general | solution.py:83
  138.4 0.9 reduce.9
  139.2 0.6 reshape.195
  139.9 6.4 %all-to-all-done.6 = bf16[64,2,256]{2,1,0:T(2,128)(2,1)S(1)} async-done(((bf16[64,2,256]{2,1,0:T(2,128)(2,1)}), bf16[64,2,256]{2,1,0:T(2,128)(2,1)S(1)}, u32[]{:S(2)}, u32[]{:S(2)}) %all-to-all-start.6) | async-done | bytes 65568 | tf_op jit(solution)/shard_map/all_to_all | solution.py:30
  146.3 4.4 %all-to-all-start.5 = ((bf16[64,2,128]{2,1,0:T(2,128)(2,1)}), bf16[64,2,128]{2,1,0:T(2,128)(2,1)S(1)}, u32[]{:S(2)}, u32[]{:S(2)}) async-start(bf16[64,2,128]{2,1,0:T(2,128)(2,1)} %reshape.195), calls=%async_computation.5 | async-start | bytes 65536 | tf_op jit(solution)/shard_map/all_to_all | solution.py:44
  150.7 0.4 convolution_convert_fusion
  151.1 1.0 copy.30
  152.2 7.9 %all-to-all-done.5 = bf16[64,2,128]{2,1,0:T(2,128)(2,1)S(1)} async-done(((bf16[64,2,128]{2,1,0:T(2,128)(2,1)}), bf16[64,2,128]{2,1,0:T(2,128)(2,1)S(1)}, u32[]{:S(2)}, u32[]{:S(2)}) %all-to-all-start.5) | async-done | bytes 32800 | tf_op jit(solution)/shard_map/all_to_all | solution.py:44
  160.1 0.7 broadcast_in_dim.11
  160.8 4.7 %all-to-all-start.7 = ((bf16[64,2,256]{2,1,0:T(2,128)(2,1)}), bf16[64,2,256]{2,1,0:T(2,128)(2,1)S(1)}, u32[]{:S(2)}, u32[]{:S(2)}) async-start(bf16[64,2,256]{2,1,0:T(2,128)(2,1)} %broadcast_in_dim.11), calls=%async_computation.7 | async-start | bytes 131072 | tf_op jit(solution)/shard_map/all_to_all | solution.py:44
  165.5 0.9 convolution_convert_fusion.3
  166.4 0.6 reduce_sum.76
  167.1 0.6 copy.39
  167.7 7.9 %all-to-all-done.7 = bf16[64,2,256]{2,1,0:T(2,128)(2,1)S(1)} async-done(((bf16[64,2,256]{2,1,0:T(2,128)(2,1)}), bf16[64,2,256]{2,1,0:T(2,128)(2,1)S(1)}, u32[]{:S(2)}, u32[]{:S(2)}) %all-to-all-start.7) | async-done | bytes 65568 | tf_op jit(solution)/shard_map/all_to_all | solution.py:44
  175.6 0.7 reshape.182
  (38 shorter events, 6.6 us)
Async XLA Ops:
  0.6 12.7 %copy-start = (bf16[1,16,64,256]{3,2,1,0:T(8,128)(2,1)S(1)}, bf16[1,16,64,256]{3,2,1,0:T(8,128)(2,1)}, u32[]{:S(2)}) copy-start(bf16[1,16,64,256]{3,2,1,0:T(8,128)(2,1)} %param.9) | copy-start | bytes 1572868
  1.5 5.3 %collective-permute-start = (bf16[1,1,64,256]{3,2,1,0:T(8,128)(2,1)S(1)}, bf16[1,1,64,256]{3,2,1,0:T(8,128)(2,1)S(1)}, u32[]{:S(2)}, u32[]{:S(2)}) collective-permute-start(bf16[1,1,64,256]{3,2,1,0:T(8,128)(2,1)S(1)} %get-tuple-element.20), channel_id=1, source_target_pairs={{0,1},{1,2},{2,3},{3,4},{4,5},{5,6},{6,7},{8,9},{9,10},{10,11},{11... | collective-permute-start | bytes 98312 | tf_op jit(solution)/shard_map/ppermute | solution.py:17
  5.5 4.7 %collective-permute-start.1 = (bf16[1,1,64,256]{3,2,1,0:T(8,128)(2,1)S(1)}, bf16[1,1,64,256]{3,2,1,0:T(8,128)(2,1)S(1)}, u32[]{:S(2)}, u32[]{:S(2)}) collective-permute-start(bf16[1,1,64,256]{3,2,1,0:T(8,128)(2,1)S(1)} %get-tuple-element.21), channel_id=1, source_target_pairs={{1,0},{2,1},{3,2},{4,3},{5,4},{6,5},{7,6},{9,8},{10,9},{11,10},{12... | collective-permute-start | bytes 98312 | tf_op jit(solution)/shard_map/ppermute | solution.py:18
  11.4 1.3 copy-start.2
  13.4 1.0 copy-start.1
  19.5 1.0 copy-start.3
  31.9 28.5 %all-to-all-start.2 = ((bf16[32,40,256]{2,1,0:T(8,128)(2,1)}), bf16[32,40,256]{2,1,0:T(8,128)(2,1)S(1)}, u32[]{:S(2)}, u32[]{:S(2)}) async-start(bf16[32,40,256]{2,1,0:T(8,128)(2,1)} %reduce_sum.74), calls=%async_computation.2 | async-start | bytes 1310720 | tf_op jit(solution)/shard_map/all_to_all | solution.py:38
  61.5 34.3 %all-to-all-start = ((bf16[8,1,8,32,256]{4,3,2,1,0:T(8,128)(2,1)}), bf16[8,1,8,32,256]{4,3,2,1,0:T(8,128)(2,1)S(1)}, u32[]{:S(2)}, u32[]{:S(2)}) async-start(bf16[8,1,8,32,256]{4,3,2,1,0:T(8,128)(2,1)} %broadcast_in_dim.8), calls=%async_computation | async-start | bytes 2097152 | tf_op jit(solution)/shard_map/all_to_all | solution.py:44
  96.6 13.4 %all-to-all-start.3 = ((f32[8,40,256]{2,1,0:T(8,128)}), f32[8,40,256]{2,1,0:T(8,128)S(1)}, u32[]{:S(2)}, u32[]{:S(2)}) async-start(f32[8,40,256]{2,1,0:T(8,128)} %broadcast_in_dim.9), calls=%async_computation.3 | async-start | bytes 655360 | tf_op jit(solution)/shard_map/all_to_all | solution.py:44
  103.2 18.9 %copy-start.4 = (bf16[1,32,16,128]{3,2,1,0:T(8,128)(2,1)S(1)}, bf16[1,32,16,128]{3,2,1,0:T(8,128)(2,1)}, u32[]{:S(2)}) copy-start(bf16[1,32,16,128]{3,2,1,0:T(8,128)(2,1)} %param.13) | copy-start | bytes 393220
  109.9 21.5 %all-to-all-start.4 = ((bf16[64,2,128]{2,1,0:T(2,128)(2,1)}), bf16[64,2,128]{2,1,0:T(2,128)(2,1)S(1)}, u32[]{:S(2)}, u32[]{:S(2)}) async-start(bf16[64,2,128]{2,1,0:T(2,128)(2,1)} %reshape.193), calls=%async_computation.4 | async-start | bytes 65536 | tf_op jit(solution)/shard_map/all_to_all | solution.py:30
  122.3 28.4 %copy-start.6 = (bf16[64,256]{1,0:T(8,128)(2,1)S(1)}, bf16[64,256]{1,0:T(8,128)(2,1)}, u32[]{:S(2)}) copy-start(bf16[64,256]{1,0:T(8,128)(2,1)} %param.16) | copy-start | bytes 98308
  131.4 14.8 %all-to-all-start.6 = ((bf16[64,2,256]{2,1,0:T(2,128)(2,1)}), bf16[64,2,256]{2,1,0:T(2,128)(2,1)S(1)}, u32[]{:S(2)}, u32[]{:S(2)}) async-start(bf16[64,2,256]{2,1,0:T(2,128)(2,1)} %reshape.180), calls=%async_computation.6 | async-start | bytes 131072 | tf_op jit(solution)/shard_map/all_to_all | solution.py:30
  138.4 27.2 %copy-start.5 = (bf16[128,256]{1,0:T(8,128)(2,1)S(1)}, bf16[128,256]{1,0:T(8,128)(2,1)}, u32[]{:S(2)}) copy-start(bf16[128,256]{1,0:T(8,128)(2,1)} %param.17) | copy-start | bytes 196612
  146.3 13.9 %all-to-all-start.5 = ((bf16[64,2,128]{2,1,0:T(2,128)(2,1)}), bf16[64,2,128]{2,1,0:T(2,128)(2,1)S(1)}, u32[]{:S(2)}, u32[]{:S(2)}) async-start(bf16[64,2,128]{2,1,0:T(2,128)(2,1)} %reshape.195), calls=%async_computation.5 | async-start | bytes 65536 | tf_op jit(solution)/shard_map/all_to_all | solution.py:44
  160.8 14.8 %all-to-all-start.7 = ((bf16[64,2,256]{2,1,0:T(2,128)(2,1)}), bf16[64,2,256]{2,1,0:T(2,128)(2,1)S(1)}, u32[]{:S(2)}, u32[]{:S(2)}) async-start(bf16[64,2,256]{2,1,0:T(2,128)(2,1)} %broadcast_in_dim.11), calls=%async_computation.7 | async-start | bytes 131072 | tf_op jit(solution)/shard_map/all_to_all | solution.py:44
where the time goes:
time: 177 us; the launch traced here: 176 us
  waiting for transfers between devices  81 us (46%)
  starting transfers between devices  51.5 us (29%)
  local copies, waits for them, and re-layouts  12.7 us (7%)
  matrix products  11.5 us (6%)
  blocking collectives  9.67 us (5%)
  other arithmetic  8.84 us (5%)
    all_to_all x4, waiting for transfers between devices, sent_to_all(): lax.all_to_all(jnp.broadcast_to(value[None], (count, *value.shape)), axis...  45.6 us
    all_to_all x4, starting transfers between devices, sent_to_all(): lax.all_to_all(jnp.broadcast_to(value[None], (count, *value.shape)), axis...  19.6 us
    all_to_all x1, waiting for transfers between devices, sum_by_axis(): lax.all_to_all(own.astype(jnp.bfloat16), far, 0, 0, tiled=True)  17.3 us
    all_to_all x2, starting transfers between devices, sum_at_owner(): lax.all_to_all(cut_along(value, dim, count), axis, 0, 0, tiled=True)  16.9 us
    all_to_all x2, waiting for transfers between devices, sum_at_owner(): lax.all_to_all(cut_along(value, dim, count), axis, 0, 0, tiled=True)  14.8 us
    all_to_all x1, starting transfers between devices, sum_by_axis(): lax.all_to_all(own.astype(jnp.bfloat16), far, 0, 0, tiled=True)  9.73 us
    all_to_all x1, blocking collectives, sum_at_owner(): lax.all_to_all(cut_along(value, dim, count), axis, 0, 0, tiled=True)  9.67 us
    dot_general x12, matrix products, contract_last(): lax.dot_general(left, right, (((1,), (1,)), ((), ())), preferred_element_...  6.32 us
  transfers between devices with their start and end apart: 9, of which 8 were waited for; matrix products, arithmetic and copies ran while one was open for 10% of the time, Pallas kernels for 0%

commit v1 on v0

v1 whole, which is shorter than its diff:
```python
import jax
import jax.numpy as jnp
from jax import lax
from jax.experimental import pallas as pl
from jax.experimental.pallas import tpu as pltpu
from jax.sharding import Mesh
from jax.sharding import PartitionSpec as P

DP = ("dp_0", "dp_1", "dp_2")
MESH = pl.DeviceIdType.MESH
F32 = jnp.float32
BF16 = jnp.bfloat16
NZ, NX, NC, NY = 8, 4, 2, 8
STRIP, WIDTH, CH = 16, 64, 256
CELLS = STRIP * WIDTH
PIECES = 4
PIECE = CELLS // 4 // PIECES


def nt(left, right):
    return lax.dot_general(left, right, (((1,), (1,)), ((), ())), preferred_element_type=F32)


def tn(left, right):
    return lax.dot_general(left, right, (((0,), (0,)), ((), ())), preferred_element_type=F32)


def nn(left, right):
    return lax.dot_general(left, right, (((1,), (0,)), ((), ())), preferred_element_type=F32)


def kernel(
    fl, og, fi, mi, ti, sw, fw, mw, tw,
    gf_o, gm_o, gt_o, kg_o, ml_o, tl_o,
    fl_v, g_v, fi_v, mi_v, ti_v, sw_v, fw_v, mw_v, tw_v,
    big, wt, flt, lvl, tmp, fg, gf_v, gath, top, gm_v, gt_v, macc,
    term, crecv, csum, xrecv, zsend, zrecv, yex, kown, kswap, kg_v,
    bterm, brecv, bsum, bxrecv, bz, bfin, bout,
    in_sem, out_sem, halo_s, halo_r, r_s, r_r, l_s, l_r,
    core_s, core_r, x_s, x_r, z_s, z_r, y_s, y_r, k_s, k_r,
    bc_s, bc_r, bx_s, bx_r, bz_s, bz_r, bf_s, bf_r,
):
    z = lax.axis_index("dp_0")
    x = lax.axis_index("dp_1")
    c = lax.axis_index("dp_2")
    y = lax.axis_index("rows")

    def remote(src, dst, send, recv, **where):
        return pltpu.make_async_remote_copy(
            src_ref=src, dst_ref=dst, send_sem=send, recv_sem=recv,
            device_id=where, device_id_type=MESH,
        )

    loads = [
        pltpu.make_async_copy(og, g_v.at[pl.ds(64, CELLS)], in_sem.at[0]),
        pltpu.make_async_copy(sw, sw_v, in_sem.at[1]),
        pltpu.make_async_copy(fl, fl_v, in_sem.at[2]),
        pltpu.make_async_copy(fi, fi_v, in_sem.at[3]),
        pltpu.make_async_copy(fw, fw_v, in_sem.at[4]),
        pltpu.make_async_copy(mi, mi_v, in_sem.at[5]),
        pltpu.make_async_copy(ti, ti_v, in_sem.at[6]),
        pltpu.make_async_copy(mw, mw_v, in_sem.at[7]),
        pltpu.make_async_copy(tw, tw_v, in_sem.at[8]),
    ]
    for load in loads:
        load.start()

    barrier = pltpu.get_barrier_semaphore()

    def greet(**where):
        pl.semaphore_signal(barrier, inc=1, device_id=where, device_id_type=MESH)

    greet(dp_2=1 - c)
    for d in range(1, NX):
        greet(dp_1=lax.rem(x + d, NX))
        greet(dp_1=lax.rem(x + d, NX), dp_2=1 - c)
    for d in range(1, NZ):
        greet(dp_0=lax.rem(z + d, NZ))
    for d in range(1, NY):
        greet(rows=lax.rem(y + d, NY))

    def widen(first, rows):
        value = g_v[pl.ds(first, rows), :].astype(F32)
        column = lax.rem(lax.broadcasted_iota(jnp.int32, (rows, CH), 0), WIDTH)
        after = jnp.where(column == WIDTH - 1, 0.0, pltpu.roll(value, rows - 1, 0))
        before = jnp.where(column == 0, 0.0, pltpu.roll(value, 1, 0))
        big[pl.ds(first, rows), 0:CH] = after.astype(BF16)
        big[pl.ds(first, rows), CH : 2 * CH] = value.astype(BF16)
        big[pl.ds(first, rows), 2 * CH : 3 * CH] = before.astype(BF16)

    loads[0].wait()

    @pl.loop(0, 4)
    def _(t):
        widen(pl.multiple_of(64 + t * 256, 64), 256)

    loads[1].wait()

    @pl.loop(0, 9)
    def _(k):
        wt[pl.ds(pl.multiple_of(k * CH, CH), CH), :] = sw_v[k].T

    pl.semaphore_wait(barrier, 1 + 2 * (NX - 1) + NZ - 1 + NY - 1)

    down = lax.rem(y + 1, NY)
    up = lax.rem(y + NY - 1, NY)
    halo_down = remote(
        g_v.at[pl.ds(CELLS, 64)], g_v.at[pl.ds(0, 64)], halo_s.at[0], halo_r.at[0], rows=down
    )
    halo_up = remote(
        g_v.at[pl.ds(64, 64)], g_v.at[pl.ds(CELLS + 64, 64)], halo_s.at[1], halo_r.at[1], rows=up
    )
    halo_down.start()
    halo_up.start()

    def ring(h, p, to_down):
        origin = lax.rem(y + NY - (h - 1), NY) if to_down else lax.rem(y + (h - 1), NY)
        block = gath.at[origin, pl.ds(pl.multiple_of(p * PIECE, PIECE), PIECE)]
        send, recv = (r_s, r_r) if to_down else (l_s, l_r)
        return remote(
            block, block, send.at[h - 1, p], recv.at[h - 1, p], rows=down if to_down else up
        )

    def arrived(h, p, from_up):
        origin = lax.rem(y + NY - h, NY) if from_up else lax.rem(y + h, NY)
        block = gath.at[origin, pl.ds(pl.multiple_of(p * PIECE, PIECE), PIECE)]
        send, recv = (r_s, r_r) if from_up else (l_s, l_r)
        return remote(
            block, block, send.at[h - 1, p], recv.at[h - 1, p], rows=down if from_up else up
        )

    def conv(t):
        first = pl.multiple_of(t * 256, 256)
        total = nn(big[pl.ds(first + 128, 256), :], wt[0:768, :])
        total = total + nn(big[pl.ds(first + 64, 256), :], wt[768:1536, :])
        total = total + nn(big[pl.ds(first, 256), :], wt[1536:2304, :])
        fg[pl.ds(first, 256), :] = total.astype(BF16)
        for j in range(2):
            half = total[:, 128 * j : 128 * j + 128]
            lvl[j, 0:64, :] = half[0:64] + half[64:128]
            lvl[j, 64:128, :] = half[128:192] + half[192:256]
            gath[y, pl.ds(pl.multiple_of(t * PIECE, PIECE), PIECE), 128 * j : 128 * j + 128] = (
                lvl[j, pl.ds(0, 64, stride=2), :] + lvl[j, pl.ds(1, 64, stride=2), :]
            ).astype(BF16)

    @pl.loop(1, 3)
    def _(t):
        conv(t)
        ring(1, t, True).start()
        ring(1, t, False).start()

    halo_down.wait_recv()
    halo_up.wait_recv()

    @pl.when(y == 0)
    def _():
        g_v[0:64, :] = jnp.zeros((64, CH), BF16)

    @pl.when(y == NY - 1)
    def _():
        g_v[CELLS + 64 : CELLS + 128, :] = jnp.zeros((64, CH), BF16)

    widen(0, 64)
    widen(CELLS + 64, 64)

    @pl.loop(0, 2)
    def _(i):
        conv(3 * i)
        ring(1, 3 * i, True).start()
        ring(1, 3 * i, False).start()

    def swap_core(k):
        rows = pl.ds(pl.multiple_of(k * CH, CH), CH)
        return remote(
            term.at[1 - c, rows], crecv.at[rows], core_s.at[k], core_r.at[k], dp_2=1 - c
        )

    def put_term(k, value):
        rows = pl.ds(pl.multiple_of(k * CH, CH), CH)
        value = value.astype(BF16)
        term[0, rows, :] = value[:, 0:128]
        term[1, rows, :] = value[:, 128:256]
        swap_core(k).start()

    def tap(k):
        row = pl.multiple_of((2 - k // 3) * 64, 64)
        col = pl.multiple_of(lax.rem(k, 3) * CH, CH)
        put_term(k, nn(flt[...], big[pl.ds(row, CELLS), pl.ds(col, CH)]))

    def step(h):
        for p in range(PIECES):
            arrived(h, p, True).wait_recv()
            if h < 3 or p < 2:
                ring(h + 1, p, True).start()
            arrived(h, p, False).wait_recv()
            if h < 3 or p >= 2:
                ring(h + 1, p, False).start()

    def coarse(s):
        mid = gath[s]
        cells = pl.ds(pl.multiple_of(s * CH, CH), CH)
        gm_v[cells, :] = nt(mid, mw_v[...]).astype(BF16)
        macc[0:64, :] += tn(mi_v[cells, :], mid)
        wide = mid.astype(F32)
        for j in range(2):
            half = wide[:, 128 * j : 128 * j + 128]
            for i in range(4):
                tmp[j, 32 * i : 32 * i + 32, :] = (
                    half[64 * i : 64 * i + 32] + half[64 * i + 32 : 64 * i + 64]
                )
            top[:, 128 * j : 128 * j + 128] = (
                tmp[j, pl.ds(0, 64, stride=2), :] + tmp[j, pl.ds(1, 64, stride=2), :]
            ).astype(BF16)
        small = top[...]
        cells = pl.ds(pl.multiple_of(s * 64, 64), 64)
        gt_v[cells, :] = nt(small, tw_v[...]).astype(BF16)
        macc[64:192, :] += tn(ti_v[cells, :], small)

    loads[2].wait()

    @pl.loop(0, 4)
    def _(t):
        rows = pl.ds(pl.multiple_of(t * 256, 256), 256)
        flt[:, rows] = fl_v[rows, :].T

    @pl.loop(0, 5)
    def _(k):
        tap(k)

    step(1)

    @pl.loop(5, 9)
    def _(k):
        tap(k)

    loads[3].wait()
    put_term(9, tn(fi_v[...], fg[...]))

    for load in loads[4:]:
        load.wait()
    macc[...] = jnp.zeros_like(macc)
    coarse(y)
    step(2)

    @pl.loop(0, 10)
    def _(k):
        swap_core(k).wait_recv()
        rows = pl.ds(pl.multiple_of(k * CH, CH), CH)
        csum[rows, :] = (term[c, rows, :].astype(F32) + crecv[rows, :].astype(F32)).astype(BF16)

    def x_copy(s, d):
        z_to = lax.rem(z + s + 1, NZ)
        x_to = lax.rem(x + d, NX)
        rows = pl.ds(pl.multiple_of((z_to * NX + x_to) * 80, 80), 80)
        return remote(
            csum.at[rows], xrecv.at[s, d - 1], x_s.at[s, d - 1], x_r.at[s, d - 1], dp_1=x_to
        )

    @pl.loop(0, NZ)
    def _(s):
        for d in range(1, NX):
            x_copy(s, d).start()

    coarse(lax.rem(y + 1, NY))
    coarse(lax.rem(y + NY - 1, NY))
    step(3)

    def z_copy(s):
        return remote(
            zsend.at[s], zrecv.at[s], z_s.at[s], z_r.at[s], dp_0=lax.rem(z + s + 1, NZ)
        )

    def x_reduce(s):
        for d in range(1, NX):
            x_copy(s, d).wait_recv()
        z_to = lax.rem(z + s + 1, NZ)
        rows = pl.ds(pl.multiple_of((z_to * NX + x) * 80, 80), 80)
        total = csum[rows, :].astype(F32)
        for d in range(1, NX):
            total = total + xrecv[s, d - 1].astype(F32)
        zsend[s] = total.astype(BF16)

    @pl.loop(0, NZ - 1)
    def _(s):
        x_reduce(s)
        z_copy(s).start()

    x_reduce(NZ - 1)

    for k in range(4):
        rows = slice(256 * k, 256 * k + 256)
        gf_v[rows, :] = nt(fg[rows, :], fw_v[...]).astype(BF16)
    stores = [pltpu.make_async_copy(gf_v, gf_o, out_sem.at[0])]
    stores[0].start()

    coarse(lax.rem(y + 2, NY))
    coarse(lax.rem(y + NY - 2, NY))
    coarse(lax.rem(y + 3, NY))
    coarse(lax.rem(y + NY - 3, NY))

    for p in range(2):
        arrived(4, p, True).wait_recv()
        arrived(4, p + 2, False).wait_recv()
    coarse(lax.rem(y + 4, NY))

    stores.append(pltpu.make_async_copy(gm_v, gm_o, out_sem.at[1]))
    stores.append(pltpu.make_async_copy(gt_v, gt_o, out_sem.at[2]))
    stores[1].start()
    stores[2].start()

    bterm[0] = macc[:, 0:128].astype(BF16)
    bterm[1] = macc[:, 128:256].astype(BF16)
    b_core = remote(bterm.at[1 - c], brecv, bc_s.at[0], bc_r.at[0], dp_2=1 - c)
    b_core.start()

    @pl.loop(0, NZ - 1)
    def _(s):
        z_copy(s).wait_recv()

    total = zsend[NZ - 1].astype(F32)
    for s in range(NZ - 1):
        total = total + zrecv[s].astype(F32)
    yex[y] = total.astype(BF16)

    def y_copy(d):
        return remote(
            yex.at[y], yex.at[y], y_s.at[d - 1], y_r.at[d - 1], rows=lax.rem(y + d, NY)
        )

    def y_arrived(d):
        block = yex.at[lax.rem(y + NY - d, NY)]
        return remote(
            block, block, y_s.at[d - 1], y_r.at[d - 1], rows=lax.rem(y + d, NY)
        )

    for d in range(1, NY):
        y_copy(d).start()

    b_core.wait_recv()
    bsum[...] = (bterm[c].astype(F32) + brecv[...].astype(F32)).astype(BF16)

    def bx_copy(d):
        x_to = lax.rem(x + d, NX)
        rows = pl.ds(pl.multiple_of(x_to * 48, 48), 48)
        return remote(bsum.at[rows], bxrecv.at[d - 1], bx_s.at[d - 1], bx_r.at[d - 1], dp_1=x_to)

    for d in range(1, NX):
        bx_copy(d).start()
    for d in range(1, NX):
        bx_copy(d).wait_recv()
    total = bsum[pl.ds(pl.multiple_of(x * 48, 48), 48), :].astype(F32)
    for d in range(1, NX):
        total = total + bxrecv[d - 1].astype(F32)
    bz[z] = total.astype(BF16)

    def bz_copy(d):
        return remote(bz.at[z], bz.at[z], bz_s.at[d - 1], bz_r.at[d - 1], dp_0=lax.rem(z + d, NZ))

    def bz_arrived(d):
        block = bz.at[lax.rem(z + NZ - d, NZ)]
        return remote(block, block, bz_s.at[d - 1], bz_r.at[d - 1], dp_0=lax.rem(z + d, NZ))

    for d in range(1, NZ):
        bz_copy(d).start()

    for d in range(1, NY):
        y_arrived(d).wait_recv()
    total = yex[0].astype(F32)
    for i in range(1, NY):
        total = total + yex[i].astype(F32)
    kown[...] = total
    k_copy = remote(
        kown.at[pl.ds(pl.multiple_of((1 - c) * 40, 8), 40)], kswap, k_s.at[0], k_r.at[0], dp_2=1 - c
    )
    k_copy.start()

    for d in range(1, NZ):
        bz_arrived(d).wait_recv()
    total = bz[0].astype(F32)
    for i in range(1, NZ):
        total = total + bz[i].astype(F32)
    bfin[x, c] = total.astype(BF16)

    def bf_copy(d, e):
        return remote(
            bfin.at[x, c], bfin.at[x, c], bf_s.at[d, e], bf_r.at[d, e],
            dp_1=lax.rem(x + d, NX), dp_2=lax.rem(c + e, NC),
        )

    def bf_arrived(d, e):
        block = bfin.at[lax.rem(x + NX - d, NX), lax.rem(c + e, NC)]
        return remote(
            block, block, bf_s.at[d, e], bf_r.at[d, e],
            dp_1=lax.rem(x + d, NX), dp_2=lax.rem(c + e, NC),
        )

    others = [(d, e) for d in range(NX) for e in range(NC) if d or e]
    for d, e in others:
        bf_copy(d, e).start()

    k_copy.wait_recv()
    kg_v[:, pl.ds(pl.multiple_of(c * 128, 128), 128)] = kown[
        pl.ds(pl.multiple_of(c * 40, 8), 40), :
    ]
    kg_v[:, pl.ds(pl.multiple_of((1 - c) * 128, 128), 128)] = kswap[...]
    stores.append(pltpu.make_async_copy(kg_v, kg_o, out_sem.at[3]))
    stores[3].start()

    for d, e in others:
        bf_arrived(d, e).wait_recv()
    for i in range(NX):
        for j in range(NC):
            bout[48 * i : 48 * i + 48, 128 * j : 128 * j + 128] = bfin[i, j].astype(F32)
    stores.append(pltpu.make_async_copy(bout.at[0:64], ml_o, out_sem.at[4]))
    stores.append(pltpu.make_async_copy(bout.at[64:192], tl_o, out_sem.at[5]))
    stores[4].start()
    stores[5].start()

    halo_down.wait_send()
    halo_up.wait_send()
    for h in range(1, 5):
        for p in range(PIECES):
            if h < 4 or p < 2:
                ring(h, p, True).wait_send()
            if h < 4 or p >= 2:
                ring(h, p, False).wait_send()

    @pl.loop(0, 10)
    def _(k):
        swap_core(k).wait_send()

    @pl.loop(0, NZ)
    def _(s):
        for d in range(1, NX):
            x_copy(s, d).wait_send()

    @pl.loop(0, NZ - 1)
    def _(s):
        z_copy(s).wait_send()

    for d in range(1, NY):
        y_copy(d).wait_send()
    b_core.wait_send()
    for d in range(1, NX):
        bx_copy(d).wait_send()
    for d in range(1, NZ):
        bz_copy(d).wait_send()
    k_copy.wait_send()
    for d, e in others:
        bf_copy(d, e).wait_send()
    for store in stores:
        store.wait()


def body(
    fine_level, out_grad, fine_input, mid_input, top_input,
    smooth_weight, fine_lateral, mid_lateral, top_lateral,
):
    sem = pltpu.SemaphoreType.DMA
    sizes = [
        ((CELLS, CH), BF16), ((CELLS + 128, CH), BF16), ((CELLS, CH), BF16), ((2048, 64), BF16),
        ((512, 128), BF16), ((9, CH, CH), BF16), ((CH, CH), BF16), ((64, CH), BF16), ((128, CH), BF16),
        ((CELLS + 128, 3 * CH), BF16), ((9 * CH, CH), BF16), ((CH, CELLS), BF16),
        ((2, 128, 128), F32), ((2, 128, 128), F32), ((CELLS, CH), BF16), ((CELLS, CH), BF16),
        ((NY, CH, CH), BF16), ((64, CH), BF16), ((2048, 64), BF16), ((512, 128), BF16), ((192, CH), F32),
        ((2, 2560, 128), BF16), ((2560, 128), BF16), ((2560, 128), BF16), ((NZ, NX - 1, 80, 128), BF16),
        ((NZ, 80, 128), BF16), ((NZ - 1, 80, 128), BF16), ((NY, 80, 128), BF16), ((80, 128), F32),
        ((40, 128), F32), ((40, CH), F32),
        ((2, 192, 128), BF16), ((192, 128), BF16), ((192, 128), BF16), ((NX - 1, 48, 128), BF16),
        ((NZ, 48, 128), BF16), ((NX, NC, 48, 128), BF16), ((192, CH), F32),
    ]
    sems = [
        (9,), (6,), (2,), (2,), (4, PIECES), (4, PIECES), (4, PIECES), (4, PIECES),
        (10,), (10,), (NZ, NX - 1), (NZ, NX - 1), (NZ - 1,), (NZ - 1,), (NY - 1,), (NY - 1,), (1,), (1,),
        (1,), (1,), (NX - 1,), (NX - 1,), (NZ - 1,), (NZ - 1,), (NX, NC), (NX, NC),
    ]
    hbm = pl.BlockSpec(memory_space=pl.ANY)
    grads = pl.pallas_call(
        kernel,
        out_shape=[
            jax.ShapeDtypeStruct((CELLS, CH), BF16),
            jax.ShapeDtypeStruct((2048, 64), BF16),
            jax.ShapeDtypeStruct((512, 128), BF16),
            jax.ShapeDtypeStruct((40, CH), F32),
            jax.ShapeDtypeStruct((64, CH), F32),
            jax.ShapeDtypeStruct((128, CH), F32),
        ],
        in_specs=[hbm] * 9,
        out_specs=[hbm] * 6,
        scratch_shapes=[pltpu.VMEM(*size) for size in sizes] + [sem(size) for size in sems],
        compiler_params=pltpu.CompilerParams(
            collective_id=0, has_side_effects=True, vmem_limit_bytes=40 * 1024 * 1024
        ),
    )(
        fine_level.reshape(CELLS, CH), out_grad.reshape(CELLS, CH), fine_input.reshape(CELLS, CH),
        mid_input.reshape(2048, 64), top_input.reshape(512, 128), smooth_weight.reshape(9, CH, CH),
        fine_lateral, mid_lateral, top_lateral,
    )
    return (
        grads[0].reshape(out_grad.shape), grads[1].reshape(mid_input.shape),
        grads[2].reshape(top_input.shape), grads[3], grads[4], grads[5],
    )


def solution(mesh):
    torus = Mesh(
        mesh.devices.reshape(NZ, NX, NC, NY), ("dp_0", "dp_1", "dp_2", "rows")
    )
    return jax.shard_map(
        body,
        mesh=torus,
        in_specs=(
            P(DP, "rows", None, None), P(DP, "rows", None, None), P(DP, "rows", None, None),
            P(DP, None, None, "rows"), P(DP, None, None, "rows"),
            P(), P(), P("rows", None), P("rows", None),
        ),
        out_specs=(
            P(DP, "rows", None, None), P(DP, None, None, "rows"), P(DP, None, None, "rows"),
            P(DP, None), P("rows", None), P("rows", None),
        ),
        check_vma=False,
    )
```

time: 177 us -> 70.1 us (0.40)
  waiting for transfers between devices: 81 us -> 0 us
  Pallas kernels: 0 us -> 55.9 us
  starting transfers between devices: 51.5 us -> 0 us
  matrix products: 11.5 us -> 0 us
  blocking collectives: 9.67 us -> 0 us
  other arithmetic: 8.84 us -> 0 us
    all_to_all x7 -> x0, waiting for transfers between devices: 77.7 us -> none  [the longest x4 45.6 us: sent_to_all(): lax.all_to_all(jnp.broadcast_to(value[None], (count, *value.shape)), axis...]
    pallas_call x0 -> x1, Pallas kernels: none -> 55.9 us  [body(): pl.pallas_call(kernel, out_shape=[jax.ShapeDtypeStruct((CELLS, CH), BF16)...]
    all_to_all x7 -> x0, starting transfers between devices: 46.2 us -> none  [the longest x4 19.6 us: sent_to_all(): lax.all_to_all(jnp.broadcast_to(value[None], (count, *value.shape)), axis...]
    dot_general x24 -> x0, matrix products: 11.5 us -> none  [the longest x12 6.32 us: contract_last(): lax.dot_general(left, right, (((1,), (1,)), ((), ())), preferred_element_...]
    all_to_all x1 -> x0, blocking collectives: 9.67 us -> none  [sum_at_owner(): lax.all_to_all(cut_along(value, dim, count), axis, 0, 0, tiled=True)]
    unnamed x19 -> x24, local copies, waits for them, and re-layouts: 4.04 us -> 13 us
    reduce_sum x7 -> x0, other arithmetic: 5.98 us -> none  [the longest x2 3.82 us: pool_two(): field.reshape(images, rows_n // 2, 2, cols_n // 2, 2, chans)]
    ppermute x2 -> x0, starting transfers between devices: 5.3 us -> none  [the longest x1 4.01 us: with_halo(): before = lax.ppermute(last, axis, up)]
  transfers between devices with their start and end apart: 9 -> 0, of which waited for: 8 -> 0; matrix products, arithmetic and copies ran while one was open for 10% -> 0% of each run, Pallas kernels for 0% -> 0%
where the time goes in v1:
time: 70.1 us; the launch traced here: 69.6 us
  Pallas kernels  55.9 us (80%)
  local copies, waits for them, and re-layouts  13 us (19%)
    pallas_call x1, Pallas kernels, body(): pl.pallas_call(kernel, out_shape=[jax.ShapeDtypeStruct((CELLS, CH), BF16)...  55.9 us
    unnamed x24, local copies, waits for them, and re-layouts  13 us

profile of v1, /device:TPU:1, one launch (start us, length us, event | category | flops | bytes accessed | tf_op | source)
XLA Modules:
  0.0 69.6 jit_solution(9973643882144086386)
XLA Ops:
  0.6 0.0 copy-start
  0.6 1.3 %copy-done = bf16[3,3,256,256]{3,2,1,0:T(8,128)(2,1)S(1)} copy-done((bf16[3,3,256,256]{3,2,1,0:T(8,128)(2,1)S(1)}, bf16[3,3,256,256]{3,2,1,0:T(8,128)(2,1)}, u32[]{:S(2)}) %copy-start) | copy-done | bytes 1179672
  1.9 0.0 copy-start.1
  1.9 1.0 %copy-done.1 = bf16[1,16,64,256]{3,2,1,0:T(8,128)(2,1)S(1)} copy-done((bf16[1,16,64,256]{3,2,1,0:T(8,128)(2,1)S(1)}, bf16[1,16,64,256]{3,2,1,0:T(8,128)(2,1)}, u32[]{:S(2)}) %copy-start.1) | copy-done | bytes 524312
  2.9 0.0 copy-start.2
  3.0 1.0 %copy-done.2 = bf16[1,16,64,256]{3,2,1,0:T(8,128)(2,1)S(1)} copy-done((bf16[1,16,64,256]{3,2,1,0:T(8,128)(2,1)S(1)}, bf16[1,16,64,256]{3,2,1,0:T(8,128)(2,1)}, u32[]{:S(2)}) %copy-start.2) | copy-done | bytes 524312
  4.0 0.0 copy-start.3
  4.0 1.0 %copy-done.3 = bf16[1,16,64,256]{3,2,1,0:T(8,128)(2,1)S(1)} copy-done((bf16[1,16,64,256]{3,2,1,0:T(8,128)(2,1)S(1)}, bf16[1,16,64,256]{3,2,1,0:T(8,128)(2,1)}, u32[]{:S(2)}) %copy-start.3) | copy-done | bytes 524312
  5.0 0.0 copy-start.4
  5.0 1.0 %copy-done.4 = bf16[1,64,32,64]{3,2,1,0:T(8,128)(2,1)S(1)} copy-done((bf16[1,64,32,64]{3,2,1,0:T(8,128)(2,1)S(1)}, bf16[1,64,32,64]{3,2,1,0:T(8,128)(2,1)}, u32[]{:S(2)}) %copy-start.4) | copy-done | bytes 262168
  6.1 0.0 copy-start.5
  6.1 0.9 %copy-done.5 = bf16[1,32,16,128]{3,2,1,0:T(8,128)(2,1)S(1)} copy-done((bf16[1,32,16,128]{3,2,1,0:T(8,128)(2,1)S(1)}, bf16[1,32,16,128]{3,2,1,0:T(8,128)(2,1)}, u32[]{:S(2)}) %copy-start.5) | copy-done | bytes 131096
  7.0 0.0 copy-start.6
  7.0 0.9 %copy-done.6 = bf16[256,256]{1,0:T(8,128)(2,1)S(1)} copy-done((bf16[256,256]{1,0:T(8,128)(2,1)S(1)}, bf16[256,256]{1,0:T(8,128)(2,1)}, u32[]{:S(2)}) %copy-start.6) | copy-done | bytes 131096
  7.9 0.0 copy-start.7
  7.9 0.8 %copy-done.7 = bf16[128,256]{1,0:T(8,128)(2,1)S(1)} copy-done((bf16[128,256]{1,0:T(8,128)(2,1)S(1)}, bf16[128,256]{1,0:T(8,128)(2,1)}, u32[]{:S(2)}) %copy-start.7) | copy-done | bytes 65560
  8.7 0.0 copy-start.8
  8.7 0.8 %copy-done.8 = bf16[64,256]{1,0:T(8,128)(2,1)S(1)} copy-done((bf16[64,256]{1,0:T(8,128)(2,1)S(1)}, bf16[64,256]{1,0:T(8,128)(2,1)}, u32[]{:S(2)}) %copy-start.8) | copy-done | bytes 32792
  9.5 55.9 %shard_map.136 = (bf16[1024,256]{1,0:T(8,128)(2,1)S(1)}, bf16[2048,64]{1,0:T(8,128)(2,1)S(1)}, bf16[512,128]{1,0:T(8,128)(2,1)S(1)}, f32[40,256]{1,0:T(8,128)S(1...) custom-call(bf16[1024,256]{1,0:T(8,128)(2,1)S(1)} %bitcast.10, bf16[1024,256]{1,0:T(8,128)(2,1)S(1)} %bitcast.11, ...), custom_call_target="tpu_custom_call" | custom-call | tf_op jit(solution)/shard_map/pallas_call | solution.py:478
  65.4 0.8 %copy.21 = bf16[1,16,64,256]{3,2,1,0:T(8,128)(2,1)} copy(bf16[1,16,64,256]{3,2,1,0:T(8,128)(2,1)S(1)} %bitcast.15) | data formatting | bytes 1048576
  66.2 0.8 %copy.22 = bf16[1,64,32,64]{3,2,1,0:T(8,128)(2,1)} copy(bf16[1,64,32,64]{3,2,1,0:T(8,128)(2,1)S(1)} %bitcast.14) | data formatting | bytes 524288
  67.0 0.7 copy.23
  67.7 0.6 copy.24
  68.3 0.6 copy.25
  68.9 0.7 copy.26
Async XLA Ops:
  0.6 1.3 %copy-start = (bf16[3,3,256,256]{3,2,1,0:T(8,128)(2,1)S(1)}, bf16[3,3,256,256]{3,2,1,0:T(8,128)(2,1)}, u32[]{:S(2)}) copy-start(bf16[3,3,256,256]{3,2,1,0:T(8,128)(2,1)} %param.14) | copy-start | bytes 3538948
  1.9 1.0 %copy-start.1 = (bf16[1,16,64,256]{3,2,1,0:T(8,128)(2,1)S(1)}, bf16[1,16,64,256]{3,2,1,0:T(8,128)(2,1)}, u32[]{:S(2)}) copy-start(bf16[1,16,64,256]{3,2,1,0:T(8,128)(2,1)} %param.9) | copy-start | bytes 1572868
  2.9 1.0 %copy-start.2 = (bf16[1,16,64,256]{3,2,1,0:T(8,128)(2,1)S(1)}, bf16[1,16,64,256]{3,2,1,0:T(8,128)(2,1)}, u32[]{:S(2)}) copy-start(bf16[1,16,64,256]{3,2,1,0:T(8,128)(2,1)} %param.10) | copy-start | bytes 1572868
  4.0 1.0 %copy-start.3 = (bf16[1,16,64,256]{3,2,1,0:T(8,128)(2,1)S(1)}, bf16[1,16,64,256]{3,2,1,0:T(8,128)(2,1)}, u32[]{:S(2)}) copy-start(bf16[1,16,64,256]{3,2,1,0:T(8,128)(2,1)} %param.11) | copy-start | bytes 1572868
  5.0 1.0 %copy-start.4 = (bf16[1,64,32,64]{3,2,1,0:T(8,128)(2,1)S(1)}, bf16[1,64,32,64]{3,2,1,0:T(8,128)(2,1)}, u32[]{:S(2)}) copy-start(bf16[1,64,32,64]{3,2,1,0:T(8,128)(2,1)} %param.12) | copy-start | bytes 786436
  6.1 0.9 %copy-start.5 = (bf16[1,32,16,128]{3,2,1,0:T(8,128)(2,1)S(1)}, bf16[1,32,16,128]{3,2,1,0:T(8,128)(2,1)}, u32[]{:S(2)}) copy-start(bf16[1,32,16,128]{3,2,1,0:T(8,128)(2,1)} %param.13) | copy-start | bytes 393220
  7.0 0.9 %copy-start.6 = (bf16[256,256]{1,0:T(8,128)(2,1)S(1)}, bf16[256,256]{1,0:T(8,128)(2,1)}, u32[]{:S(2)}) copy-start(bf16[256,256]{1,0:T(8,128)(2,1)} %fw.1) | copy-start | bytes 393220
  7.9 0.8 %copy-start.7 = (bf16[128,256]{1,0:T(8,128)(2,1)S(1)}, bf16[128,256]{1,0:T(8,128)(2,1)}, u32[]{:S(2)}) copy-start(bf16[128,256]{1,0:T(8,128)(2,1)} %tw.1) | copy-start | bytes 196612
  8.7 0.8 %copy-start.8 = (bf16[64,256]{1,0:T(8,128)(2,1)S(1)}, bf16[64,256]{1,0:T(8,128)(2,1)}, u32[]{:S(2)}) copy-start(bf16[64,256]{1,0:T(8,128)(2,1)} %mw.1) | copy-start | bytes 98308

commit v2 on v1

--- a/solution.py
+++ b/solution.py
@@ -13,8 +13,9 @@
 NZ, NX, NC, NY = 8, 4, 2, 8
 STRIP, WIDTH, CH = 16, 64, 256
 CELLS = STRIP * WIDTH
-PIECES = 4
-PIECE = CELLS // 4 // PIECES
+PIECES = ((32, 64), (96, 64), (160, 64), (0, 32), (224, 32))
+INNER, EDGES = (0, 1, 2), (3, 4)
+LAST_DOWN, LAST_UP = (0, 1), (2, 3, 4)
 
 
 def nt(left, right):
@@ -35,10 +36,10 @@
     fl_v, g_v, fi_v, mi_v, ti_v, sw_v, fw_v, mw_v, tw_v,
     big, wt, flt, lvl, tmp, fg, gf_v, gath, top, gm_v, gt_v, macc,
     term, crecv, csum, xrecv, zsend, zrecv, yex, kown, kswap, kg_v,
-    bterm, brecv, bsum, bxrecv, bz, bfin, bout,
+    bterm, bxrecv, bz, bfin, bout,
     in_sem, out_sem, halo_s, halo_r, r_s, r_r, l_s, l_r,
     core_s, core_r, x_s, x_r, z_s, z_r, y_s, y_r, k_s, k_r,
-    bc_s, bc_r, bx_s, bx_r, bz_s, bz_r, bf_s, bf_r,
+    bx_s, bx_r, bz_s, bz_r, bf_s, bf_r,
 ):
     z = lax.axis_index("dp_0")
     x = lax.axis_index("dp_1")
@@ -62,7 +63,7 @@
         pltpu.make_async_copy(mw, mw_v, in_sem.at[7]),
         pltpu.make_async_copy(tw, tw_v, in_sem.at[8]),
     ]
-    for load in loads:
+    for load in loads[:3]:
         load.start()
 
     barrier = pltpu.get_barrier_semaphore()
@@ -99,6 +100,9 @@
     @pl.loop(0, 9)
     def _(k):
         wt[pl.ds(pl.multiple_of(k * CH, CH), CH), :] = sw_v[k].T
+
+    for load in loads[3:]:
+        load.start()
 
     pl.semaphore_wait(barrier, 1 + 2 * (NX - 1) + NZ - 1 + NY - 1)
 
@@ -113,61 +117,50 @@
     halo_down.start()
     halo_up.start()
 
-    def ring(h, p, to_down):
-        origin = lax.rem(y + NY - (h - 1), NY) if to_down else lax.rem(y + (h - 1), NY)
-        block = gath.at[origin, pl.ds(pl.multiple_of(p * PIECE, PIECE), PIECE)]
+    def hop(h, p, to_down, sent):
+        away = h - 1 if sent else h
+        origin = lax.rem(y + NY - away, NY) if to_down else lax.rem(y + away, NY)
+        first, count = PIECES[p] if isinstance(p, int) else (pl.multiple_of(32 + 64 * p, 32), 64)
+        block = gath.at[origin, pl.ds(first, count)]
         send, recv = (r_s, r_r) if to_down else (l_s, l_r)
         return remote(
             block, block, send.at[h - 1, p], recv.at[h - 1, p], rows=down if to_down else up
         )
 
-    def arrived(h, p, from_up):
-        origin = lax.rem(y + NY - h, NY) if from_up else lax.rem(y + h, NY)
-        block = gath.at[origin, pl.ds(pl.multiple_of(p * PIECE, PIECE), PIECE)]
-        send, recv = (r_s, r_r) if from_up else (l_s, l_r)
-        return remote(
-            block, block, send.at[h - 1, p], recv.at[h - 1, p], rows=down if from_up else up
-        )
-
-    def conv(t):
-        first = pl.multiple_of(t * 256, 256)
-        total = nn(big[pl.ds(first + 128, 256), :], wt[0:768, :])
-        total = total + nn(big[pl.ds(first + 64, 256), :], wt[768:1536, :])
-        total = total + nn(big[pl.ds(first, 256), :], wt[1536:2304, :])
-        fg[pl.ds(first, 256), :] = total.astype(BF16)
+    def start_own(p):
+        hop(1, p, True, True).start()
+        hop(1, p, False, True).start()
+
+    def goes(h, p, to_down):
+        return h < 4 or p in (LAST_DOWN if to_down else LAST_UP)
+
+    def forward(h, pieces):
+        for p in pieces:
+            for to_down in (True, False):
+                if goes(h, p, to_down):
+                    hop(h, p, to_down, False).wait_recv()
+                if h < 4 and goes(h + 1, p, to_down):
+                    hop(h + 1, p, to_down, True).start()
+
+    def conv(first, cells, out):
+        total = nn(big[pl.ds(first + 128, cells), :], wt[0:768, :])
+        total = total + nn(big[pl.ds(first + 64, cells), :], wt[768:1536, :])
+        total = total + nn(big[pl.ds(first, cells), :], wt[1536:2304, :])
+        fg[pl.ds(first, cells), :] = total.astype(BF16)
         for j in range(2):
             half = total[:, 128 * j : 128 * j + 128]
-            lvl[j, 0:64, :] = half[0:64] + half[64:128]
-            lvl[j, 64:128, :] = half[128:192] + half[192:256]
-            gath[y, pl.ds(pl.multiple_of(t * PIECE, PIECE), PIECE), 128 * j : 128 * j + 128] = (
-                lvl[j, pl.ds(0, 64, stride=2), :] + lvl[j, pl.ds(1, 64, stride=2), :]
+            for i in range(cells // 128):
+                lvl[j, 64 * i : 64 * i + 64, :] = (
+                    half[128 * i : 128 * i + 64] + half[128 * i + 64 : 128 * i + 128]
+                )
+            gath[y, pl.ds(out, cells // 4), 128 * j : 128 * j + 128] = (
+                lvl[j, pl.ds(0, cells // 4, stride=2), :] + lvl[j, pl.ds(1, cells // 4, stride=2), :]
             ).astype(BF16)
 
-    @pl.loop(1, 3)
+    @pl.loop(0, 3)
     def _(t):
-        conv(t)
-        ring(1, t, True).start()
-        ring(1, t, False).start()
-
-    halo_down.wait_recv()
-    halo_up.wait_recv()
-
-    @pl.when(y == 0)
-    def _():
-        g_v[0:64, :] = jnp.zeros((64, CH), BF16)
-
-    @pl.when(y == NY - 1)
-    def _():
-        g_v[CELLS + 64 : CELLS + 128, :] = jnp.zeros((64, CH), BF16)
-
-    widen(0, 64)
-    widen(CELLS + 64, 64)
-
-    @pl.loop(0, 2)
-    def _(i):
-        conv(3 * i)
-        ring(1, 3 * i, True).start()
-        ring(1, 3 * i, False).start()
+        conv(pl.multiple_of(128 + 256 * t, 128), 256, pl.multiple_of(32 + 64 * t, 32))
+        start_own(t)
 
     def swap_core(k):
         rows = pl.ds(pl.multiple_of(k * CH, CH), CH)
@@ -187,14 +180,47 @@
         col = pl.multiple_of(lax.rem(k, 3) * CH, CH)
         put_term(k, nn(flt[...], big[pl.ds(row, CELLS), pl.ds(col, CH)]))
 
-    def step(h):
-        for p in range(PIECES):
-            arrived(h, p, True).wait_recv()
-            if h < 3 or p < 2:
-                ring(h + 1, p, True).start()
-            arrived(h, p, False).wait_recv()
-            if h < 3 or p >= 2:
-                ring(h + 1, p, False).start()
+    loads[2].wait()
+
+    @pl.loop(0, 4)
+    def _(t):
+        rows = pl.ds(pl.multiple_of(t * 256, 256), 256)
+        flt[:, rows] = fl_v[rows, :].T
+
+    @pl.loop(3, 6)
+    def _(k):
+        tap(k)
+
+    halo_down.wait_recv()
+    halo_up.wait_recv()
+
+    @pl.when(y == 0)
+    def _():
+        g_v[0:64, :] = jnp.zeros((64, CH), BF16)
+
+    @pl.when(y == NY - 1)
+    def _():
+        g_v[CELLS + 64 : CELLS + 128, :] = jnp.zeros((64, CH), BF16)
+
+    widen(0, 64)
+    widen(CELLS + 64, 64)
+
+    for p in EDGES:
+        first, count = PIECES[p]
+        conv(4 * first, 4 * count, first)
+        start_own(p)
+
+    forward(1, INNER)
+
+    @pl.loop(0, 3)
+    def _(k):
+        tap(k)
+
+    forward(1, EDGES)
+
+    @pl.loop(6, 9)
+    def _(k):
+        tap(k)
 
     def coarse(s):
         mid = gath[s]
@@ -216,23 +242,6 @@
         gt_v[cells, :] = nt(small, tw_v[...]).astype(BF16)
         macc[64:192, :] += tn(ti_v[cells, :], small)
 
-    loads[2].wait()
-
-    @pl.loop(0, 4)
-    def _(t):
-        rows = pl.ds(pl.multiple_of(t * 256, 256), 256)
-        flt[:, rows] = fl_v[rows, :].T
-
-    @pl.loop(0, 5)
-    def _(k):
-        tap(k)
-
-    step(1)
-
-    @pl.loop(5, 9)
-    def _(k):
-        tap(k)
-
     loads[3].wait()
     put_term(9, tn(fi_v[...], fg[...]))
 
@@ -240,7 +249,7 @@
         load.wait()
     macc[...] = jnp.zeros_like(macc)
     coarse(y)
-    step(2)
+    forward(2, INNER)
 
     @pl.loop(0, 10)
     def _(k):
@@ -263,7 +272,11 @@
 
     coarse(lax.rem(y + 1, NY))
     coarse(lax.rem(y + NY - 1, NY))
-    step(3)
+    forward(2, EDGES)
+    coarse(lax.rem(y + 2, NY))
+    coarse(lax.rem(y + NY - 2, NY))
+    forward(3, INNER)
+    forward(3, EDGES)
 
     def z_copy(s):
         return remote(
@@ -293,14 +306,10 @@
     stores = [pltpu.make_async_copy(gf_v, gf_o, out_sem.at[0])]
     stores[0].start()
 
-    coarse(lax.rem(y + 2, NY))
-    coarse(lax.rem(y + NY - 2, NY))
     coarse(lax.rem(y + 3, NY))
     coarse(lax.rem(y + NY - 3, NY))
 
-    for p in range(2):
-        arrived(4, p, True).wait_recv()
-        arrived(4, p + 2, False).wait_recv()
+    forward(4, INNER + EDGES)
     coarse(lax.rem(y + 4, NY))
 
     stores.append(pltpu.make_async_copy(gm_v, gm_o, out_sem.at[1]))
@@ -308,10 +317,37 @@
     stores[1].start()
     stores[2].start()
 
-    bterm[0] = macc[:, 0:128].astype(BF16)
-    bterm[1] = macc[:, 128:256].astype(BF16)
-    b_core = remote(bterm.at[1 - c], brecv, bc_s.at[0], bc_r.at[0], dp_2=1 - c)
-    b_core.start()
+    others = [(d, e) for d in range(NX) for e in range(NC) if d or e]
+    for i in range(NX):
+        for j in range(NC):
+            bterm[i, j] = macc[48 * i : 48 * i + 48, 128 * j : 128 * j + 128].astype(BF16)
+
+    def bx_copy(d, e):
+        x_to, c_to = lax.rem(x + d, NX), lax.rem(c + e, NC)
+        return remote(
+            bterm.at[x_to, c_to], bxrecv.at[d, e], bx_s.at[d, e], bx_r.at[d, e],
+            dp_1=x_to, dp_2=c_to,
+        )
+
+    for d, e in others:
+        bx_copy(d, e).start()
+
+    for d, e in others:
+        bx_copy(d, e).wait_recv()
+    total = bterm[x, c].astype(F32)
+    for d, e in others:
+        total = total + bxrecv[d, e].astype(F32)
+    bz[z] = total.astype(BF16)
+
+    def bz_copy(d):
+        return remote(bz.at[z], bz.at[z], bz_s.at[d - 1], bz_r.at[d - 1], dp_0=lax.rem(z + d, NZ))
+
+    def bz_arrived(d):
+        block = bz.at[lax.rem(z + NZ - d, NZ)]
+        return remote(block, block, bz_s.at[d - 1], bz_r.at[d - 1], dp_0=lax.rem(z + d, NZ))
+
+    for d in range(1, NZ):
+        bz_copy(d).start()
 
     @pl.loop(0, NZ - 1)
     def _(s):
@@ -335,33 +371,6 @@
 
     for d in range(1, NY):
         y_copy(d).start()
-
-    b_core.wait_recv()
-    bsum[...] = (bterm[c].astype(F32) + brecv[...].astype(F32)).astype(BF16)
-
-    def bx_copy(d):
-        x_to = lax.rem(x + d, NX)
-        rows = pl.ds(pl.multiple_of(x_to * 48, 48), 48)
-        return remote(bsum.at[rows], bxrecv.at[d - 1], bx_s.at[d - 1], bx_r.at[d - 1], dp_1=x_to)
-
-    for d in range(1, NX):
-        bx_copy(d).start()
-    for d in range(1, NX):
-        bx_copy(d).wait_recv()
-    total = bsum[pl.ds(pl.multiple_of(x * 48, 48), 48), :].astype(F32)
-    for d in range(1, NX):
-        total = total + bxrecv[d - 1].astype(F32)
-    bz[z] = total.astype(BF16)
-
-    def bz_copy(d):
-        return remote(bz.at[z], bz.at[z], bz_s.at[d - 1], bz_r.at[d - 1], dp_0=lax.rem(z + d, NZ))
-
-    def bz_arrived(d):
-        block = bz.at[lax.rem(z + NZ - d, NZ)]
-        return remote(block, block, bz_s.at[d - 1], bz_r.at[d - 1], dp_0=lax.rem(z + d, NZ))
-
-    for d in range(1, NZ):
-        bz_copy(d).start()
 
     for d in range(1, NY):
         y_arrived(d).wait_recv()
@@ -394,7 +403,6 @@
             dp_1=lax.rem(x + d, NX), dp_2=lax.rem(c + e, NC),
         )
 
-    others = [(d, e) for d in range(NX) for e in range(NC) if d or e]
     for d, e in others:
         bf_copy(d, e).start()
 
@@ -419,11 +427,10 @@
     halo_down.wait_send()
     halo_up.wait_send()
     for h in range(1, 5):
-        for p in range(PIECES):
-            if h < 4 or p < 2:
-                ring(h, p, True).wait_send()
-            if h < 4 or p >= 2:
-                ring(h, p, False).wait_send()
+        for p in range(len(PIECES)):
+            for to_down in (True, False):
+                if goes(h, p, to_down):
+                    hop(h, p, to_down, True).wait_send()
 
     @pl.loop(0, 10)
     def _(k):
@@ -440,9 +447,8 @@
 
     for d in range(1, NY):
         y_copy(d).wait_send()
-    b_core.wait_send()
-    for d in range(1, NX):
-        bx_copy(d).wait_send()
+    for d, e in others:
+        bx_copy(d, e).wait_send()
     for d in range(1, NZ):
         bz_copy(d).wait_send()
     k_copy.wait_send()
@@ -450,6 +456,14 @@
         bf_copy(d, e).wait_send()
     for store in stores:
         store.wait()
+
+
+def store(*refs):
+    copies = [pltpu.make_async_copy(refs[i], refs[6 + i], refs[12].at[i]) for i in range(6)]
+    for copy in copies:
+        copy.start()
+    for copy in copies:
+        copy.wait()
 
 
 def body(
@@ -466,36 +480,41 @@
         ((2, 2560, 128), BF16), ((2560, 128), BF16), ((2560, 128), BF16), ((NZ, NX - 1, 80, 128), BF16),
         ((NZ, 80, 128), BF16), ((NZ - 1, 80, 128), BF16), ((NY, 80, 128), BF16), ((80, 128), F32),
         ((40, 128), F32), ((40, CH), F32),
-        ((2, 192, 128), BF16), ((192, 128), BF16), ((192, 128), BF16), ((NX - 1, 48, 128), BF16),
+        ((NX, NC, 48, 128), BF16), ((NX, NC, 48, 128), BF16),
         ((NZ, 48, 128), BF16), ((NX, NC, 48, 128), BF16), ((192, CH), F32),
     ]
     sems = [
-        (9,), (6,), (2,), (2,), (4, PIECES), (4, PIECES), (4, PIECES), (4, PIECES),
+        (9,), (6,), (2,), (2,), (4, 5), (4, 5), (4, 5), (4, 5),
         (10,), (10,), (NZ, NX - 1), (NZ, NX - 1), (NZ - 1,), (NZ - 1,), (NY - 1,), (NY - 1,), (1,), (1,),
-        (1,), (1,), (NX - 1,), (NX - 1,), (NZ - 1,), (NZ - 1,), (NX, NC), (NX, NC),
+        (NX, NC), (NX, NC), (NZ - 1,), (NZ - 1,), (NX, NC), (NX, NC),
     ]
-    hbm = pl.BlockSpec(memory_space=pl.ANY)
+    shapes = [
+        ((CELLS, CH), BF16), ((2048, 64), BF16), ((512, 128), BF16),
+        ((40, CH), F32), ((64, CH), F32), ((128, CH), F32),
+    ]
+    hbm = pl.BlockSpec(memory_space=pltpu.HBM)
+    anywhere = pl.BlockSpec(memory_space=pl.ANY)
     grads = pl.pallas_call(
         kernel,
-        out_shape=[
-            jax.ShapeDtypeStruct((CELLS, CH), BF16),
-            jax.ShapeDtypeStruct((2048, 64), BF16),
-            jax.ShapeDtypeStruct((512, 128), BF16),
-            jax.ShapeDtypeStruct((40, CH), F32),
-            jax.ShapeDtypeStruct((64, CH), F32),
-            jax.ShapeDtypeStruct((128, CH), F32),
-        ],
+        out_shape=[pltpu.VMEM(*shape) for shape in shapes],
         in_specs=[hbm] * 9,
-        out_specs=[hbm] * 6,
+        out_specs=[anywhere] * 6,
         scratch_shapes=[pltpu.VMEM(*size) for size in sizes] + [sem(size) for size in sems],
         compiler_params=pltpu.CompilerParams(
-            collective_id=0, has_side_effects=True, vmem_limit_bytes=40 * 1024 * 1024
+            collective_id=0, has_side_effects=True, vmem_limit_bytes=48 * 1024 * 1024
         ),
-    )(
+    )(*(pltpu.with_memory_space_constraint(value, pltpu.HBM) for value in (
         fine_level.reshape(CELLS, CH), out_grad.reshape(CELLS, CH), fine_input.reshape(CELLS, CH),
         mid_input.reshape(2048, 64), top_input.reshape(512, 128), smooth_weight.reshape(9, CH, CH),
         fine_lateral, mid_lateral, top_lateral,
-    )
+    )))
+    grads = pl.pallas_call(
+        store,
+        out_shape=[pltpu.HBM(*shape) for shape in shapes],
+        in_specs=[anywhere] * 6,
+        out_specs=[hbm] * 6,
+        scratch_shapes=[sem((6,))],
+    )(*(pltpu.with_memory_space_constraint(grad, pltpu.VMEM) for grad in grads))
     return (
         grads[0].reshape(out_grad.shape), grads[1].reshape(mid_input.shape),
         grads[2].reshape(top_input.shape), grads[3], grads[4], grads[5],

time: 70.1 us -> 55.7 us (0.79)
  local copies, waits for them, and re-layouts: 13 us -> 0 us
  Pallas kernels: 55.9 us -> 54.9 us
    unnamed x24 -> x0, local copies, waits for them, and re-layouts: 13 us -> none
    pallas_call x1 -> x2, Pallas kernels: 55.9 us -> 54.9 us  [the longest x1 53.7 us: body(): pl.pallas_call(kernel, out_shape=[pltpu.VMEM(*shape) for shape in shapes]...]
where the time goes in v2:
time: 55.7 us; the launch traced here: 55.5 us
  Pallas kernels  54.9 us (99%)
  between operations  0.64 us (1%)
    pallas_call x1, Pallas kernels, body(): pl.pallas_call(kernel, out_shape=[pltpu.VMEM(*shape) for shape in shapes]...  53.7 us
    pallas_call x1, Pallas kernels, body(): pl.pallas_call(store, out_shape=[pltpu.HBM(*shape) for shape in shapes],...  1.13 us

profile of v2, /device:TPU:1, one launch (start us, length us, event | category | flops | bytes accessed | tf_op | source)
XLA Modules:
  0.0 55.5 jit_solution(14235844637477614130)
XLA Ops:
  0.6 53.7 %shard_map.136 = (bf16[1024,256]{1,0:T(8,128)(2,1)S(1)}, bf16[2048,64]{1,0:T(8,128)(2,1)S(1)}, bf16[512,128]{1,0:T(8,128)(2,1)S(1)}, f32[40,256]{1,0:T(8,128)S(1...) custom-call(bf16[1024,256]{1,0:T(8,128)(2,1)} %bitcast.10, bf16[1024,256]{1,0:T(8,128)(2,1)} %bitcast.11, ...), custom_call_target="tpu_custom_call" | custom-call | tf_op jit(solution)/shard_map/pallas_call | solution.py:497
  54.4 1.1 %shard_map.137 = (bf16[1024,256]{1,0:T(8,128)(2,1)}, bf16[2048,64]{1,0:T(8,128)(2,1)}, bf16[512,128]{1,0:T(8,128)(2,1)}, f32[40,256]{1,0:T(8,128)}, f32[64,256]{1,0:T(8,128)}, /*index=5*/f32[128,256]{1,0:T(8,128)}) custom-call(bf16[1024,256]{1,0:T(8,128)(2,1)S(1)} %get-tuple-element.18.refs_0_, bf16[2048,64]{1,0:T(8,128)(2,1)S(1)} %get-tuple-element.19.refs_1_, ...), custom_call_target="tpu_custom_call" | custom-call | tf_op jit(solution)/shard_map/pallas_call | solution.py:511

commit v3 on v2

--- a/solution.py
+++ b/solution.py
@@ -40,6 +40,7 @@
     in_sem, out_sem, halo_s, halo_r, r_s, r_r, l_s, l_r,
     core_s, core_r, x_s, x_r, z_s, z_r, y_s, y_r, k_s, k_r,
     bx_s, bx_r, bz_s, bz_r, bf_s, bf_r,
+    seen_y, seen_z, seen_x, seen_c,
 ):
     z = lax.axis_index("dp_0")
     x = lax.axis_index("dp_1")
@@ -71,14 +72,33 @@
     def greet(**where):
         pl.semaphore_signal(barrier, inc=1, device_id=where, device_id_type=MESH)
 
-    greet(dp_2=1 - c)
-    for d in range(1, NX):
-        greet(dp_1=lax.rem(x + d, NX))
-        greet(dp_1=lax.rem(x + d, NX), dp_2=1 - c)
-    for d in range(1, NZ):
-        greet(dp_0=lax.rem(z + d, NZ))
-    for d in range(1, NY):
-        greet(rows=lax.rem(y + d, NY))
+    down, up = lax.rem(y + 1, NY), lax.rem(y + NY - 1, NY)
+    x_next, x_last = lax.rem(x + 1, NX), lax.rem(x + NX - 1, NX)
+    z_next, z_last = lax.rem(z + 1, NZ), lax.rem(z + NZ - 1, NZ)
+    for where in (
+        dict(rows=down), dict(rows=up), dict(dp_1=x_next), dict(dp_1=x_last),
+        dict(dp_0=z_next), dict(dp_0=z_last), dict(dp_2=1 - c),
+    ):
+        greet(**where)
+
+    def tell(r):
+        def pair(sem, nexts, lasts):
+            pl.semaphore_signal(sem.at[0], inc=1, device_id=nexts, device_id_type=MESH)
+            pl.semaphore_signal(sem.at[1], inc=1, device_id=lasts, device_id_type=MESH)
+
+        pair(seen_y, dict(rows=down), dict(rows=up))
+        pair(seen_z, dict(dp_0=z_next), dict(dp_0=z_last))
+        if r == 1:
+            pair(seen_x, dict(dp_1=x_next), dict(dp_1=x_last))
+        if r == 2:
+            pl.semaphore_signal(seen_c.at[0], inc=1, device_id=dict(dp_2=1 - c), device_id_type=MESH)
+
+    def hear(r):
+        for sem in (seen_y, seen_z) + ((seen_x,) if r == 1 else ()):
+            pl.semaphore_wait(sem.at[0], 1)
+            pl.semaphore_wait(sem.at[1], 1)
+        if r == 2:
+            pl.semaphore_wait(seen_c.at[0], 1)
 
     def widen(first, rows):
         value = g_v[pl.ds(first, rows), :].astype(F32)
@@ -95,19 +115,8 @@
     def _(t):
         widen(pl.multiple_of(64 + t * 256, 64), 256)
 
-    loads[1].wait()
-
-    @pl.loop(0, 9)
-    def _(k):
-        wt[pl.ds(pl.multiple_of(k * CH, CH), CH), :] = sw_v[k].T
-
-    for load in loads[3:]:
-        load.start()
-
-    pl.semaphore_wait(barrier, 1 + 2 * (NX - 1) + NZ - 1 + NY - 1)
-
-    down = lax.rem(y + 1, NY)
-    up = lax.rem(y + NY - 1, NY)
+    pl.semaphore_wait(barrier, 7)
+
     halo_down = remote(
         g_v.at[pl.ds(CELLS, 64)], g_v.at[pl.ds(0, 64)], halo_s.at[0], halo_r.at[0], rows=down
     )
@@ -117,6 +126,14 @@
     halo_down.start()
     halo_up.start()
 
+    tell(1)
+
+    loads[1].wait()
+
+    @pl.loop(0, 9)
+    def _(k):
+        wt[pl.ds(pl.multiple_of(k * CH, CH), CH), :] = sw_v[k].T
+
     def hop(h, p, to_down, sent):
         away = h - 1 if sent else h
         origin = lax.rem(y + NY - away, NY) if to_down else lax.rem(y + away, NY)
@@ -142,24 +159,56 @@
                 if h < 4 and goes(h + 1, p, to_down):
                     hop(h + 1, p, to_down, True).start()
 
-    def conv(first, cells, out):
-        total = nn(big[pl.ds(first + 128, cells), :], wt[0:768, :])
-        total = total + nn(big[pl.ds(first + 64, cells), :], wt[768:1536, :])
-        total = total + nn(big[pl.ds(first, cells), :], wt[1536:2304, :])
-        fg[pl.ds(first, cells), :] = total.astype(BF16)
+    def conv(rows):
+        total = nn(rows(128), wt[0:768, :])
+        total = total + nn(rows(64), wt[768:1536, :])
+        return total + nn(rows(0), wt[1536:2304, :])
+
+    def pool(total, put):
         for j in range(2):
             half = total[:, 128 * j : 128 * j + 128]
-            for i in range(cells // 128):
+            for i in range(2):
                 lvl[j, 64 * i : 64 * i + 64, :] = (
                     half[128 * i : 128 * i + 64] + half[128 * i + 64 : 128 * i + 128]
                 )
-            gath[y, pl.ds(out, cells // 4), 128 * j : 128 * j + 128] = (
-                lvl[j, pl.ds(0, cells // 4, stride=2), :] + lvl[j, pl.ds(1, cells // 4, stride=2), :]
-            ).astype(BF16)
+            put(
+                j,
+                (lvl[j, pl.ds(0, 64, stride=2), :] + lvl[j, pl.ds(1, 64, stride=2), :]).astype(BF16),
+            )
+
+    def conv_inner(t):
+        first = pl.multiple_of(128 + 256 * t, 128)
+        out = pl.multiple_of(32 + 64 * t, 32)
+        total = conv(lambda shift: big[pl.ds(first + shift, 256), :])
+        fg[pl.ds(first, 256), :] = total.astype(BF16)
+
+        def put(j, pooled):
+            gath[y, pl.ds(out, 64), 128 * j : 128 * j + 128] = pooled
+
+        pool(total, put)
+
+    def conv_edges():
+        low = CELLS - 128
+        total = conv(
+            lambda shift: jnp.concatenate(
+                [big[shift : shift + 128, :], big[low + shift : low + shift + 128, :]]
+            )
+        )
+        fg[0:128, :] = total[0:128].astype(BF16)
+        fg[low:CELLS, :] = total[128:256].astype(BF16)
+
+        def put(j, pooled):
+            gath[y, 0:32, 128 * j : 128 * j + 128] = pooled[0:32]
+            gath[y, 224:256, 128 * j : 128 * j + 128] = pooled[32:64]
+
+        pool(total, put)
+
+    for load in loads[3:]:
+        load.start()
 
     @pl.loop(0, 3)
     def _(t):
-        conv(pl.multiple_of(128 + 256 * t, 128), 256, pl.multiple_of(32 + 64 * t, 32))
+        conv_inner(t)
         start_own(t)
 
     def swap_core(k):
@@ -205,9 +254,8 @@
     widen(0, 64)
     widen(CELLS + 64, 64)
 
+    conv_edges()
     for p in EDGES:
-        first, count = PIECES[p]
-        conv(4 * first, 4 * count, first)
         start_own(p)
 
     forward(1, INNER)
@@ -216,11 +264,14 @@
     def _(k):
         tap(k)
 
-    forward(1, EDGES)
+    hear(1)
+    tell(2)
 
     @pl.loop(6, 9)
     def _(k):
         tap(k)
+
+    forward(1, EDGES)
 
     def coarse(s):
         mid = gath[s]
@@ -242,63 +293,79 @@
         gt_v[cells, :] = nt(small, tw_v[...]).astype(BF16)
         macc[64:192, :] += tn(ti_v[cells, :], small)
 
+    def core_sum(k):
+        swap_core(k).wait_recv()
+        rows = pl.ds(pl.multiple_of(k * CH, CH), CH)
+        csum[rows, :] = (term[c, rows, :].astype(F32) + crecv[rows, :].astype(F32)).astype(BF16)
+
+    def owner(s):
+        return 4 * (s // 4) + lax.rem(z + s + 1, 4)
+
+    def x_copy(s, d):
+        x_to = lax.rem(x + d, NX)
+        rows = pl.ds(pl.multiple_of((owner(s) * NX + x_to) * 80, 80), 80)
+        return remote(
+            csum.at[rows], xrecv.at[s, d - 1], x_s.at[s, d - 1], x_r.at[s, d - 1], dp_1=x_to
+        )
+
+    def x_send(batch):
+        @pl.loop(5 * batch, 5 * batch + 5)
+        def _(k):
+            core_sum(k)
+
+        @pl.loop(4 * batch, 4 * batch + 4)
+        def _(s):
+            for d in range(1, NX):
+                x_copy(s, d).start()
+
+    def z_copy(z_to):
+        slot = lax.rem(z_to - z + NZ, NZ) - 1
+        return remote(zsend.at[z_to], zrecv.at[slot], z_s.at[slot], z_r.at[slot], dp_0=z_to)
+
+    def x_reduce(batch):
+        @pl.loop(4 * batch, 4 * batch + 4)
+        def _(s):
+            for d in range(1, NX):
+                x_copy(s, d).wait_recv()
+            z_to = owner(s)
+            rows = pl.ds(pl.multiple_of((z_to * NX + x) * 80, 80), 80)
+            total = csum[rows, :].astype(F32)
+            for d in range(1, NX):
+                total = total + xrecv[s, d - 1].astype(F32)
+            zsend[z_to] = total.astype(BF16)
+
+            @pl.when(z_to != z)
+            def _():
+                z_copy(z_to).start()
+
+    def z_arrived(d):
+        block = zrecv.at[d - 1]
+        return remote(block, block, z_s.at[d - 1], z_r.at[d - 1], dp_0=lax.rem(z + d, NZ))
+
+    x_send(0)
+
     loads[3].wait()
     put_term(9, tn(fi_v[...], fg[...]))
+
+    forward(2, INNER)
 
     for load in loads[4:]:
         load.wait()
     macc[...] = jnp.zeros_like(macc)
     coarse(y)
-    forward(2, INNER)
-
-    @pl.loop(0, 10)
-    def _(k):
-        swap_core(k).wait_recv()
-        rows = pl.ds(pl.multiple_of(k * CH, CH), CH)
-        csum[rows, :] = (term[c, rows, :].astype(F32) + crecv[rows, :].astype(F32)).astype(BF16)
-
-    def x_copy(s, d):
-        z_to = lax.rem(z + s + 1, NZ)
-        x_to = lax.rem(x + d, NX)
-        rows = pl.ds(pl.multiple_of((z_to * NX + x_to) * 80, 80), 80)
-        return remote(
-            csum.at[rows], xrecv.at[s, d - 1], x_s.at[s, d - 1], x_r.at[s, d - 1], dp_1=x_to
-        )
-
-    @pl.loop(0, NZ)
-    def _(s):
-        for d in range(1, NX):
-            x_copy(s, d).start()
-
     coarse(lax.rem(y + 1, NY))
     coarse(lax.rem(y + NY - 1, NY))
+
+    x_send(1)
+
+    hear(2)
+    tell(3)
     forward(2, EDGES)
+
+    forward(3, INNER)
+
     coarse(lax.rem(y + 2, NY))
     coarse(lax.rem(y + NY - 2, NY))
-    forward(3, INNER)
-    forward(3, EDGES)
-
-    def z_copy(s):
-        return remote(
-            zsend.at[s], zrecv.at[s], z_s.at[s], z_r.at[s], dp_0=lax.rem(z + s + 1, NZ)
-        )
-
-    def x_reduce(s):
-        for d in range(1, NX):
-            x_copy(s, d).wait_recv()
-        z_to = lax.rem(z + s + 1, NZ)
-        rows = pl.ds(pl.multiple_of((z_to * NX + x) * 80, 80), 80)
-        total = csum[rows, :].astype(F32)
-        for d in range(1, NX):
-            total = total + xrecv[s, d - 1].astype(F32)
-        zsend[s] = total.astype(BF16)
-
-    @pl.loop(0, NZ - 1)
-    def _(s):
-        x_reduce(s)
-        z_copy(s).start()
-
-    x_reduce(NZ - 1)
 
     for k in range(4):
         rows = slice(256 * k, 256 * k + 256)
@@ -306,16 +373,17 @@
     stores = [pltpu.make_async_copy(gf_v, gf_o, out_sem.at[0])]
     stores[0].start()
 
+    forward(3, EDGES)
+
     coarse(lax.rem(y + 3, NY))
     coarse(lax.rem(y + NY - 3, NY))
 
+    hear(3)
+    x_reduce(0)
+
     forward(4, INNER + EDGES)
+
     coarse(lax.rem(y + 4, NY))
-
-    stores.append(pltpu.make_async_copy(gm_v, gm_o, out_sem.at[1]))
-    stores.append(pltpu.make_async_copy(gt_v, gt_o, out_sem.at[2]))
-    stores[1].start()
-    stores[2].start()
 
     others = [(d, e) for d in range(NX) for e in range(NC) if d or e]
     for i in range(NX):
@@ -331,6 +399,13 @@
 
     for d, e in others:
         bx_copy(d, e).start()
+
+    stores.append(pltpu.make_async_copy(gm_v, gm_o, out_sem.at[1]))
+    stores.append(pltpu.make_async_copy(gt_v, gt_o, out_sem.at[2]))
+    stores[1].start()
+    stores[2].start()
+
+    x_reduce(1)
 
     for d, e in others:
         bx_copy(d, e).wait_recv()
@@ -349,13 +424,11 @@
     for d in range(1, NZ):
         bz_copy(d).start()
 
-    @pl.loop(0, NZ - 1)
-    def _(s):
-        z_copy(s).wait_recv()
-
-    total = zsend[NZ - 1].astype(F32)
-    for s in range(NZ - 1):
-        total = total + zrecv[s].astype(F32)
+    for d in range(1, NZ):
+        z_arrived(d).wait_recv()
+    total = zsend[z].astype(F32)
+    for i in range(NZ - 1):
+        total = total + zrecv[i].astype(F32)
     yex[y] = total.astype(BF16)
 
     def y_copy(d):
@@ -365,12 +438,33 @@
 
     def y_arrived(d):
         block = yex.at[lax.rem(y + NY - d, NY)]
-        return remote(
-            block, block, y_s.at[d - 1], y_r.at[d - 1], rows=lax.rem(y + d, NY)
-        )
+        return remote(block, block, y_s.at[d - 1], y_r.at[d - 1], rows=lax.rem(y + d, NY))
 
     for d in range(1, NY):
         y_copy(d).start()
+
+    for d in range(1, NZ):
+        bz_arrived(d).wait_recv()
+    total = bz[0].astype(F32)
+    for i in range(1, NZ):
+        total = total + bz[i].astype(F32)
+    bfin[x, c] = total.astype(BF16)
+
+    def bf_copy(d, e):
+        return remote(
+            bfin.at[x, c], bfin.at[x, c], bf_s.at[d, e], bf_r.at[d, e],
+            dp_1=lax.rem(x + d, NX), dp_2=lax.rem(c + e, NC),
+        )
+
+    def bf_arrived(d, e):
+        block = bfin.at[lax.rem(x + NX - d, NX), lax.rem(c + e, NC)]
+        return remote(
+            block, block, bf_s.at[d, e], bf_r.at[d, e],
+            dp_1=lax.rem(x + d, NX), dp_2=lax.rem(c + e, NC),
+        )
+
+    for d, e in others:
+        bf_copy(d, e).start()
 
     for d in range(1, NY):
         y_arrived(d).wait_recv()
@@ -383,29 +477,6 @@
     )
     k_copy.start()
 
-    for d in range(1, NZ):
-        bz_arrived(d).wait_recv()
-    total = bz[0].astype(F32)
-    for i in range(1, NZ):
-        total = total + bz[i].astype(F32)
-    bfin[x, c] = total.astype(BF16)
-
-    def bf_copy(d, e):
-        return remote(
-            bfin.at[x, c], bfin.at[x, c], bf_s.at[d, e], bf_r.at[d, e],
-            dp_1=lax.rem(x + d, NX), dp_2=lax.rem(c + e, NC),
-        )
-
-    def bf_arrived(d, e):
-        block = bfin.at[lax.rem(x + NX - d, NX), lax.rem(c + e, NC)]
-        return remote(
-            block, block, bf_s.at[d, e], bf_r.at[d, e],
-            dp_1=lax.rem(x + d, NX), dp_2=lax.rem(c + e, NC),
-        )
-
-    for d, e in others:
-        bf_copy(d, e).start()
-
     k_copy.wait_recv()
     kg_v[:, pl.ds(pl.multiple_of(c * 128, 128), 128)] = kown[
         pl.ds(pl.multiple_of(c * 40, 8), 40), :
@@ -441,9 +512,8 @@
         for d in range(1, NX):
             x_copy(s, d).wait_send()
 
-    @pl.loop(0, NZ - 1)
-    def _(s):
-        z_copy(s).wait_send()
+    for d in range(1, NZ):
+        z_copy(lax.rem(z + d, NZ)).wait_send()
 
     for d in range(1, NY):
         y_copy(d).wait_send()
@@ -499,7 +569,8 @@
         out_shape=[pltpu.VMEM(*shape) for shape in shapes],
         in_specs=[hbm] * 9,
         out_specs=[anywhere] * 6,
-        scratch_shapes=[pltpu.VMEM(*size) for size in sizes] + [sem(size) for size in sems],
+        scratch_shapes=[pltpu.VMEM(*size) for size in sizes] + [sem(size) for size in sems]
+        + [pltpu.SemaphoreType.REGULAR((count,)) for count in (2, 2, 2, 1)],
         compiler_params=pltpu.CompilerParams(
             collective_id=0, has_side_effects=True, vmem_limit_bytes=48 * 1024 * 1024
         ),

time: 55.7 us -> 48.5 us (0.87)
  Pallas kernels: 54.9 us -> 47.7 us
    pallas_call x1, Pallas kernels: 53.7 us -> 46.6 us  [body(): pl.pallas_call(kernel, out_shape=[pltpu.VMEM(*shape) for shape in shapes]...]
where the time goes in v3:
time: 48.5 us; the launch traced here: 48.4 us
  Pallas kernels  47.7 us (98%)
  between operations  0.64 us (1%)
    pallas_call x1, Pallas kernels, body(): pl.pallas_call(kernel, out_shape=[pltpu.VMEM(*shape) for shape in shapes]...  46.6 us
    pallas_call x1, Pallas kernels, body(): pl.pallas_call(store, out_shape=[pltpu.HBM(*shape) for shape in shapes],...  1.13 us

profile of v3, /device:TPU:1, one launch (start us, length us, event | category | flops | bytes accessed | tf_op | source)
XLA Modules:
  0.0 48.4 jit_solution(4435828632059065704)
XLA Ops:
  0.6 46.6 %shard_map.136 = (bf16[1024,256]{1,0:T(8,128)(2,1)S(1)}, bf16[2048,64]{1,0:T(8,128)(2,1)S(1)}, bf16[512,128]{1,0:T(8,128)(2,1)S(1)}, f32[40,256]{1,0:T(8,128)S(1...) custom-call(bf16[1024,256]{1,0:T(8,128)(2,1)} %bitcast.10, bf16[1024,256]{1,0:T(8,128)(2,1)} %bitcast.11, ...), custom_call_target="tpu_custom_call" | custom-call | tf_op jit(solution)/shard_map/pallas_call | solution.py:567
  47.2 1.1 %shard_map.137 = (bf16[1024,256]{1,0:T(8,128)(2,1)}, bf16[2048,64]{1,0:T(8,128)(2,1)}, bf16[512,128]{1,0:T(8,128)(2,1)}, f32[40,256]{1,0:T(8,128)}, f32[64,256]{1,0:T(8,128)}, /*index=5*/f32[128,256]{1,0:T(8,128)}) custom-call(bf16[1024,256]{1,0:T(8,128)(2,1)S(1)} %get-tuple-element.18.refs_0_, bf16[2048,64]{1,0:T(8,128)(2,1)S(1)} %get-tuple-element.19.refs_1_, ...), custom_call_target="tpu_custom_call" | custom-call | tf_op jit(solution)/shard_map/pallas_call | solution.py:582

commit v4 on v3

v4 whole, which is shorter than its diff:
```python
import jax
import jax.numpy as jnp
from jax import lax
from jax.experimental import pallas as pl
from jax.experimental.pallas import tpu as pltpu
from jax.sharding import Mesh
from jax.sharding import PartitionSpec as P

DP = ("dp_0", "dp_1", "dp_2")
MESH = pl.DeviceIdType.MESH
F32 = jnp.float32
BF16 = jnp.bfloat16
NZ, NX, NC, NY = 8, 4, 2, 8
STRIP, WIDTH, CH = 16, 64, 256
CELLS = STRIP * WIDTH
PIECES = ((32, 64), (96, 64), (160, 64), (0, 32), (224, 32))
INNER, EDGES = (0, 1, 2), (3, 4)
LAST_DOWN, LAST_UP = (0, 1), (2, 3, 4)


def nt(left, right):
    return lax.dot_general(left, right, (((1,), (1,)), ((), ())), preferred_element_type=F32)


def tn(left, right):
    return lax.dot_general(left, right, (((0,), (0,)), ((), ())), preferred_element_type=F32)


def nn(left, right):
    return lax.dot_general(left, right, (((1,), (0,)), ((), ())), preferred_element_type=F32)


def kernel(
    fl, og, fi, mi, ti, sw, fw, mw, tw,
    gf_o, gm_o, gt_o, kg_o, ml_o, tl_o,
    fl_v, g_v, fi_v, mi_v, ti_v, sw_v, fw_v, mw_v, tw_v,
    big, wt, flt, lvl, tmp, fg, gath, top, macc,
    term, crecv, csum, xrecv, zsend, zrecv, yown, yex,
    bterm, bxrecv, bz, bfin,
    in_sem, halo_s, halo_r, ring_s, edge_s, ring_r, last_r,
    core_s, core_r, x_s, x_r, z_s, z_r, y_s, y_r,
    bx_s, bx_r, bz_s, bz_r, bf_s, bf_r,
    seen_y, seen_z, seen_x, seen_c,
):
    z = lax.axis_index("dp_0")
    x = lax.axis_index("dp_1")
    c = lax.axis_index("dp_2")
    y = lax.axis_index("rows")

    def remote(src, dst, send, recv, **where):
        return pltpu.make_async_remote_copy(
            src_ref=src, dst_ref=dst, send_sem=send, recv_sem=recv,
            device_id=where, device_id_type=MESH,
        )

    def wait_bytes(ref, sem):
        remote(ref, ref, sem, sem, dp_2=1 - c).wait_recv()

    loads = [
        pltpu.make_async_copy(og, g_v.at[pl.ds(64, CELLS)], in_sem.at[0]),
        pltpu.make_async_copy(sw, sw_v, in_sem.at[1]),
        pltpu.make_async_copy(fl, fl_v, in_sem.at[2]),
        pltpu.make_async_copy(fi, fi_v, in_sem.at[3]),
        pltpu.make_async_copy(fw, fw_v, in_sem.at[4]),
        pltpu.make_async_copy(mi, mi_v, in_sem.at[5]),
        pltpu.make_async_copy(ti, ti_v, in_sem.at[6]),
        pltpu.make_async_copy(mw, mw_v, in_sem.at[7]),
        pltpu.make_async_copy(tw, tw_v, in_sem.at[8]),
    ]
    for load in loads[:3]:
        load.start()

    barrier = pltpu.get_barrier_semaphore()

    def greet(**where):
        pl.semaphore_signal(barrier, inc=1, device_id=where, device_id_type=MESH)

    down, up = lax.rem(y + 1, NY), lax.rem(y + NY - 1, NY)
    x_next, x_last = lax.rem(x + 1, NX), lax.rem(x + NX - 1, NX)
    z_next, z_last = lax.rem(z + 1, NZ), lax.rem(z + NZ - 1, NZ)
    for where in (
        dict(rows=down), dict(rows=up), dict(dp_1=x_next), dict(dp_1=x_last),
        dict(dp_0=z_next), dict(dp_0=z_last), dict(dp_2=1 - c),
    ):
        greet(**where)

    def tell(sem, *others):
        for i, where in enumerate(others):
            pl.semaphore_signal(sem.at[i], inc=1, device_id=where, device_id_type=MESH)

    def hear(sem, count=2):
        for i in range(count):
            pl.semaphore_wait(sem.at[i], 1)

    def tell_y():
        tell(seen_y, dict(rows=down), dict(rows=up))

    def tell_z():
        tell(seen_z, dict(dp_0=z_next), dict(dp_0=z_last))

    def widen(first, rows):
        value = g_v[pl.ds(first, rows), :].astype(F32)
        column = lax.rem(lax.broadcasted_iota(jnp.int32, (rows, CH), 0), WIDTH)
        after = jnp.where(column == WIDTH - 1, 0.0, pltpu.roll(value, rows - 1, 0))
        before = jnp.where(column == 0, 0.0, pltpu.roll(value, 1, 0))
        big[pl.ds(first, rows), 0:CH] = after.astype(BF16)
        big[pl.ds(first, rows), CH : 2 * CH] = value.astype(BF16)
        big[pl.ds(first, rows), 2 * CH : 3 * CH] = before.astype(BF16)

    loads[0].wait()
    pl.semaphore_wait(barrier, 7)

    halo_down = remote(
        g_v.at[pl.ds(CELLS, 64)], g_v.at[pl.ds(0, 64)], halo_s.at[0], halo_r.at[0], rows=down
    )
    halo_up = remote(
        g_v.at[pl.ds(64, 64)], g_v.at[pl.ds(CELLS + 64, 64)], halo_s.at[0], halo_r.at[0], rows=up
    )
    halo_down.start()
    halo_up.start()


    @pl.loop(0, 4)
    def _(t):
        widen(pl.multiple_of(64 + t * 256, 64), 256)

    tell_y()
    tell_z()
    tell(seen_x, dict(dp_1=x_next), dict(dp_1=x_last))

    loads[1].wait()

    @pl.loop(0, 9)
    def _(k):
        wt[pl.ds(pl.multiple_of(k * CH, CH), CH), :] = sw_v[k].T

    def send_piece(p, away, stride, to_down):
        origin = lax.rem(y + NY - away, NY) if to_down else lax.rem(y + away, NY)
        target = lax.rem(y + stride, NY) if to_down else lax.rem(y + NY - stride, NY)
        first, count = PIECES[p] if isinstance(p, int) else (pl.multiple_of(32 + 64 * p, 32), 64)
        block = gath.at[origin, pl.ds(first, count)]
        h = away + stride
        group = 3 if isinstance(p, int) and p in EDGES else p
        recv = last_r.at[0] if h == 4 else ring_r.at[h - 1, group, 0 if to_down else 1]
        send = edge_s if isinstance(p, int) and p in EDGES else ring_s
        remote(block, block, send.at[0], recv, rows=target).start()

    def came(h, group, to_down):
        wait_bytes(gath.at[0, pl.ds(0, 64)], ring_r.at[h - 1, group, 0 if to_down else 1])

    def start_own(p):
        send_piece(p, 0, 1, True)
        send_piece(p, 0, 1, False)

    def forward(h, p):
        for to_down in (True, False):
            came(h, p, to_down)
            if h < 3 or p in (LAST_DOWN if to_down else LAST_UP):
                send_piece(p, h, 1, to_down)

    def edges_from_home():
        for stride in (1, 2):
            for p in EDGES:
                send_piece(p, 0, stride, True)
                send_piece(p, 0, stride, False)

    def edges_on():
        for to_down in (True, False):
            came(2, 3, to_down)
            for p in EDGES:
                send_piece(p, 2, 1, to_down)
                if p in (LAST_DOWN if to_down else LAST_UP):
                    send_piece(p, 2, 2, to_down)

    def conv(rows):
        total = nn(rows(128), wt[0:768, :])
        total = total + nn(rows(64), wt[768:1536, :])
        return total + nn(rows(0), wt[1536:2304, :])

    def pool(total, put):
        for j in range(2):
            half = total[:, 128 * j : 128 * j + 128]
            for i in range(2):
                lvl[j, 64 * i : 64 * i + 64, :] = (
                    half[128 * i : 128 * i + 64] + half[128 * i + 64 : 128 * i + 128]
                )
            put(
                j,
                (lvl[j, pl.ds(0, 64, stride=2), :] + lvl[j, pl.ds(1, 64, stride=2), :]).astype(BF16),
            )

    def conv_inner(t):
        first = pl.multiple_of(128 + 256 * t, 128)
        out = pl.multiple_of(32 + 64 * t, 32)
        total = conv(lambda shift: big[pl.ds(first + shift, 256), :])
        fg[pl.ds(first, 256), :] = total.astype(BF16)

        def put(j, pooled):
            gath[y, pl.ds(out, 64), 128 * j : 128 * j + 128] = pooled

        pool(total, put)

    def conv_edges():
        low = CELLS - 128
        total = conv(
            lambda shift: jnp.concatenate(
                [big[shift : shift + 128, :], big[low + shift : low + shift + 128, :]]
            )
        )
        fg[0:128, :] = total[0:128].astype(BF16)
        fg[low:CELLS, :] = total[128:256].astype(BF16)

        def put(j, pooled):
            gath[y, 0:32, 128 * j : 128 * j + 128] = pooled[0:32]
            gath[y, 224:256, 128 * j : 128 * j + 128] = pooled[32:64]

        pool(total, put)

    for load in loads[3:]:
        load.start()

    @pl.loop(0, 3)
    def _(t):
        conv_inner(t)
        start_own(t)

    def swap_core(k):
        rows = pl.ds(pl.multiple_of(k * CH, CH), CH)
        return remote(
            term.at[1 - c, rows], crecv.at[rows], core_s.at[0], core_r.at[k // 5], dp_2=1 - c
        )

    def put_term(k, value):
        rows = pl.ds(pl.multiple_of(k * CH, CH), CH)
        value = value.astype(BF16)
        term[0, rows, :] = value[:, 0:128]
        term[1, rows, :] = value[:, 128:256]
        swap_core(k).start()

    def tap(k):
        row = pl.multiple_of((2 - k // 3) * 64, 64)
        col = pl.multiple_of(lax.rem(k, 3) * CH, CH)
        put_term(k, nn(flt[...], big[pl.ds(row, CELLS), pl.ds(col, CH)]))

    loads[2].wait()

    @pl.loop(0, 4)
    def _(t):
        rows = pl.ds(pl.multiple_of(t * 256, 256), 256)
        flt[:, rows] = fl_v[rows, :].T

    @pl.loop(3, 6)
    def _(k):
        tap(k)

    wait_bytes(g_v.at[pl.ds(0, 128)], halo_r.at[0])

    @pl.when(y == 0)
    def _():
        g_v[0:64, :] = jnp.zeros((64, CH), BF16)

    @pl.when(y == NY - 1)
    def _():
        g_v[CELLS + 64 : CELLS + 128, :] = jnp.zeros((64, CH), BF16)

    widen(0, 64)
    widen(CELLS + 64, 64)

    conv_edges()
    hear(seen_y)
    edges_from_home()
    tell_y()

    @pl.loop(0, 3)
    def _(p):
        forward(1, p)
        tap(p)

    @pl.loop(6, 9)
    def _(k):
        tap(k)

    def coarse(s):
        mid = gath[s]
        cells = pl.ds(pl.multiple_of(s * CH, CH), CH)
        gm_o[cells, :] = nt(mid, mw_v[...]).astype(BF16)
        macc[0:64, :] += tn(mi_v[cells, :], mid)
        wide = mid.astype(F32)
        for j in range(2):
            half = wide[:, 128 * j : 128 * j + 128]
            for i in range(4):
                tmp[j, 32 * i : 32 * i + 32, :] = (
                    half[64 * i : 64 * i + 32] + half[64 * i + 32 : 64 * i + 64]
                )
            top[:, 128 * j : 128 * j + 128] = (
                tmp[j, pl.ds(0, 64, stride=2), :] + tmp[j, pl.ds(1, 64, stride=2), :]
            ).astype(BF16)
        small = top[...]
        cells = pl.ds(pl.multiple_of(s * 64, 64), 64)
        gt_o[cells, :] = nt(small, tw_v[...]).astype(BF16)
        macc[64:192, :] += tn(ti_v[cells, :], small)

    def core_sum(k):
        rows = pl.ds(pl.multiple_of(k * CH, CH), CH)
        csum[rows, :] = (term[c, rows, :].astype(F32) + crecv[rows, :].astype(F32)).astype(BF16)

    def owner(s):
        return 4 * (s // 4) + lax.rem(z + s + 1, 4)

    def x_copy(s, d):
        x_to = lax.rem(x + d, NX)
        rows = pl.ds(pl.multiple_of((owner(s) * NX + x_to) * 80, 80), 80)
        return remote(
            csum.at[rows], xrecv.at[s, d - 1], x_s.at[0], x_r.at[s], dp_1=x_to
        )

    def x_send(batch):
        wait_bytes(crecv.at[pl.ds(1280 * batch, 1280)], core_r.at[batch])

        @pl.loop(5 * batch, 5 * batch + 5)
        def _(k):
            core_sum(k)

        @pl.loop(4 * batch, 4 * batch + 4)
        def _(s):
            for d in range(1, NX):
                x_copy(s, d).start()

    def z_copy(z_to):
        slot = lax.rem(z_to - z + NZ, NZ) - 1
        return remote(zsend.at[z_to], zrecv.at[slot], z_s.at[0], z_r.at[0], dp_0=z_to)

    def x_reduce(batch):
        @pl.loop(4 * batch, 4 * batch + 4)
        def _(s):
            wait_bytes(xrecv.at[s], x_r.at[s])
            z_to = owner(s)
            rows = pl.ds(pl.multiple_of((z_to * NX + x) * 80, 80), 80)
            total = csum[rows, :].astype(F32)
            for d in range(1, NX):
                total = total + xrecv[s, d - 1].astype(F32)
            zsend[z_to] = total.astype(BF16)

            @pl.when(z_to != z)
            def _():
                z_copy(z_to).start()

    hear(seen_x)
    forward(2, 0)

    x_send(0)

    loads[3].wait()
    put_term(9, tn(fi_v[...], fg[...]))

    forward(2, 1)
    forward(2, 2)

    for load in loads[4:]:
        load.wait()
    macc[...] = jnp.zeros_like(macc)
    coarse(y)

    x_send(1)

    hear(seen_y)
    edges_on()
    tell_y()
    hear(seen_z)
    tell_z()

    came(1, 3, True)
    came(1, 3, False)
    coarse(lax.rem(y + 1, NY))
    coarse(lax.rem(y + NY - 1, NY))

    forward(3, 0)
    forward(3, 1)
    forward(3, 2)

    coarse(lax.rem(y + 2, NY))
    coarse(lax.rem(y + NY - 2, NY))

    for k in range(4):
        rows = slice(256 * k, 256 * k + 256)
        gf_o[rows, :] = nt(fg[rows, :], fw_v[...]).astype(BF16)

    hear(seen_y)
    hear(seen_z)
    tell_z()
    tell(seen_c, dict(dp_2=1 - c))

    came(3, 3, True)
    came(3, 3, False)

    coarse(lax.rem(y + 3, NY))
    coarse(lax.rem(y + NY - 3, NY))

    hear(seen_z)

    x_reduce(0)

    wait_bytes(gath.at[0], last_r.at[0])

    coarse(lax.rem(y + 4, NY))
    hear(seen_c, 1)

    others = [(d, e) for d in range(NX) for e in range(NC) if d or e]
    for i in range(NX):
        for j in range(NC):
            bterm[NC * i + j] = macc[48 * i : 48 * i + 48, 128 * j : 128 * j + 128].astype(BF16)

    def bx_copy(d, e):
        x_to, c_to = lax.rem(x + d, NX), lax.rem(c + e, NC)
        return remote(
            bterm.at[NC * x_to + c_to], bxrecv.at[NC * d + e - 1], bx_s.at[0], bx_r.at[0],
            dp_1=x_to, dp_2=c_to,
        )

    for d, e in others:
        bx_copy(d, e).start()

    x_reduce(1)

    wait_bytes(bxrecv, bx_r.at[0])
    total = bterm[NC * x + c].astype(F32)
    for i in range(NX * NC - 1):
        total = total + bxrecv[i].astype(F32)
    bz[z] = total.astype(BF16)

    def bz_copy(d):
        return remote(bz.at[z], bz.at[z], bz_s.at[0], bz_r.at[0], dp_0=lax.rem(z + d, NZ))

    for d in range(1, NZ):
        bz_copy(d).start()

    wait_bytes(zrecv, z_r.at[0])
    total = zsend[z].astype(F32)
    for i in range(NZ - 1):
        total = total + zrecv[i].astype(F32)
    for i in range(NC):
        yown[i] = total[40 * i : 40 * i + 40].astype(BF16)
    yex[NY * c + y] = yown[c]

    def y_copy(d, e):
        c_to = lax.rem(c + e, NC)
        return remote(
            yown.at[c_to], yex.at[NY * c + y], y_s.at[0], y_r.at[0],
            rows=lax.rem(y + d, NY), dp_2=c_to,
        )

    for d in range(NY):
        for e in range(NC):
            if d or e:
                y_copy(d, e).start()

    wait_bytes(bz.at[pl.ds(0, NZ - 1)], bz_r.at[0])
    total = bz[0].astype(F32)
    for i in range(1, NZ):
        total = total + bz[i].astype(F32)
    bfin[NC * x + c] = total.astype(BF16)

    def bf_copy(d, e):
        return remote(
            bfin.at[NC * x + c], bfin.at[NC * x + c], bf_s.at[0], bf_r.at[0],
            dp_1=lax.rem(x + d, NX), dp_2=lax.rem(c + e, NC),
        )

    for d, e in others:
        bf_copy(d, e).start()

    wait_bytes(yex.at[pl.ds(0, NC * NY - 1)], y_r.at[0])
    for i in range(NC):
        total = yex[NY * i].astype(F32)
        for j in range(1, NY):
            total = total + yex[NY * i + j].astype(F32)
        kg_o[:, 128 * i : 128 * i + 128] = total

    for ref, sem in (
        (g_v.at[pl.ds(0, 128)], halo_s), (gath.at[pl.ds(0, 7), pl.ds(0, 192)], ring_s),
        (gath.at[pl.ds(0, 7), pl.ds(0, 64)], edge_s), (crecv, core_s),
        (csum.at[pl.ds(0, NZ * (NX - 1) * 80)], x_s), (zrecv, z_s), (yex.at[pl.ds(0, NC * NY - 1)], y_s),
        (bxrecv, bx_s), (bz.at[pl.ds(0, NZ - 1)], bz_s),
    ):
        wait_bytes(ref, sem.at[0])

    wait_bytes(bfin.at[pl.ds(0, NX * NC - 1)], bf_r.at[0])
    for i in range(NX):
        for j in range(NC):
            block = bfin[NC * i + j].astype(F32)
            cols = slice(128 * j, 128 * j + 128)
            if i == 0:
                ml_o[0:48, cols] = block
            elif i == 1:
                ml_o[48:64, cols] = block[0:16]
                tl_o[0:32, cols] = block[16:48]
            else:
                tl_o[48 * i - 64 : 48 * i - 16, cols] = block
    wait_bytes(bfin.at[pl.ds(0, NX * NC - 1)], bf_s.at[0])


def store(*refs):
    copies = [pltpu.make_async_copy(refs[i], refs[6 + i], refs[12].at[i]) for i in range(6)]
    for copy in copies:
        copy.start()
    for copy in copies:
        copy.wait()


def body(
    fine_level, out_grad, fine_input, mid_input, top_input,
    smooth_weight, fine_lateral, mid_lateral, top_lateral,
):
    sem = pltpu.SemaphoreType.DMA
    sizes = [
        ((CELLS, CH), BF16), ((CELLS + 128, CH), BF16), ((CELLS, CH), BF16), ((2048, 64), BF16),
        ((512, 128), BF16), ((9, CH, CH), BF16), ((CH, CH), BF16), ((64, CH), BF16), ((128, CH), BF16),
        ((CELLS + 128, 3 * CH), BF16), ((9 * CH, CH), BF16), ((CH, CELLS), BF16),
        ((2, 128, 128), F32), ((2, 128, 128), F32), ((CELLS, CH), BF16),
        ((NY, CH, CH), BF16), ((64, CH), BF16), ((192, CH), F32),
        ((2, 2560, 128), BF16), ((2560, 128), BF16), ((2560, 128), BF16), ((NZ, NX - 1, 80, 128), BF16),
        ((NZ, 80, 128), BF16), ((NZ - 1, 80, 128), BF16), ((NC, 40, 128), BF16), ((NC * NY, 40, 128), BF16),
        ((NX * NC, 48, 128), BF16), ((NX * NC - 1, 48, 128), BF16),
        ((NZ, 48, 128), BF16), ((NX * NC, 48, 128), BF16),
    ]
    sems = [
        (9,), (1,), (1,), (1,), (1,), (3, 4, 2), (1,),
        (1,), (2,), (1,), (NZ,), (1,), (1,), (1,), (1,),
        (1,), (1,), (1,), (1,), (1,), (1,),
    ]
    shapes = [
        ((CELLS, CH), BF16), ((2048, 64), BF16), ((512, 128), BF16),
        ((40, CH), F32), ((64, CH), F32), ((128, CH), F32),
    ]
    hbm = pl.BlockSpec(memory_space=pltpu.HBM)
    anywhere = pl.BlockSpec(memory_space=pl.ANY)
    grads = pl.pallas_call(
        kernel,
        out_shape=[pltpu.VMEM(*shape) for shape in shapes],
        in_specs=[hbm] * 9,
        out_specs=[pl.BlockSpec(memory_space=pltpu.VMEM)] * 6,
        scratch_shapes=[pltpu.VMEM(*size) for size in sizes] + [sem(size) for size in sems]
        + [pltpu.SemaphoreType.REGULAR((count,)) for count in (2, 2, 2, 1)],
        compiler_params=pltpu.CompilerParams(
            collective_id=0, has_side_effects=True, vmem_limit_bytes=48 * 1024 * 1024
        ),
    )(*(pltpu.with_memory_space_constraint(value, pltpu.HBM) for value in (
        fine_level.reshape(CELLS, CH), out_grad.reshape(CELLS, CH), fine_input.reshape(CELLS, CH),
        mid_input.reshape(2048, 64), top_input.reshape(512, 128), smooth_weight.reshape(9, CH, CH),
        fine_lateral, mid_lateral, top_lateral,
    )))
    grads = pl.pallas_call(
        store,
        out_shape=[pltpu.HBM(*shape) for shape in shapes],
        in_specs=[anywhere] * 6,
        out_specs=[hbm] * 6,
        scratch_shapes=[sem((6,))],
    )(*(pltpu.with_memory_space_constraint(grad, pltpu.VMEM) for grad in grads))
    return (
        grads[0].reshape(out_grad.shape), grads[1].reshape(mid_input.shape),
        grads[2].reshape(top_input.shape), grads[3], grads[4], grads[5],
    )


def solution(mesh):
    torus = Mesh(
        mesh.devices.reshape(NZ, NX, NC, NY), ("dp_0", "dp_1", "dp_2", "rows")
    )
    return jax.shard_map(
        body,
        mesh=torus,
        in_specs=(
            P(DP, "rows", None, None), P(DP, "rows", None, None), P(DP, "rows", None, None),
            P(DP, None, None, "rows"), P(DP, None, None, "rows"),
            P(), P(), P("rows", None), P("rows", None),
        ),
        out_specs=(
            P(DP, "rows", None, None), P(DP, None, None, "rows"), P(DP, None, None, "rows"),
            P(DP, None), P("rows", None), P("rows", None),
        ),
        check_vma=False,
    )
```

time: 48.5 us -> 46 us (0.948)
  Pallas kernels: 47.7 us -> 45.2 us
    pallas_call x1, Pallas kernels: 46.6 us -> 44 us  [body(): pl.pallas_call(kernel, out_shape=[pltpu.VMEM(*shape) for shape in shapes]...]
where the time goes in v4:
time: 46 us; the launch traced here: 45.8 us
  Pallas kernels  45.2 us (98%)
  between operations  0.64 us (1%)
    pallas_call x1, Pallas kernels, body(): pl.pallas_call(kernel, out_shape=[pltpu.VMEM(*shape) for shape in shapes]...  44 us
    pallas_call x1, Pallas kernels, body(): pl.pallas_call(store, out_shape=[pltpu.HBM(*shape) for shape in shapes],...  1.13 us

profile of v4, /device:TPU:1, one launch (start us, length us, event | category | flops | bytes accessed | tf_op | source)
XLA Modules:
  0.0 45.8 jit_solution(12267131072762142979)
XLA Ops:
  0.6 44.0 %shard_map.136 = (bf16[1024,256]{1,0:T(8,128)(2,1)S(1)}, bf16[2048,64]{1,0:T(8,128)(2,1)S(1)}, bf16[512,128]{1,0:T(8,128)(2,1)S(1)}, f32[40,256]{1,0:T(8,128)S(1...) custom-call(bf16[1024,256]{1,0:T(8,128)(2,1)} %bitcast.10, bf16[1024,256]{1,0:T(8,128)(2,1)} %bitcast.11, ...), custom_call_target="tpu_custom_call" | custom-call | tf_op jit(solution)/shard_map/pallas_call | solution.py:537
  44.7 1.1 %shard_map.137 = (bf16[1024,256]{1,0:T(8,128)(2,1)}, bf16[2048,64]{1,0:T(8,128)(2,1)}, bf16[512,128]{1,0:T(8,128)(2,1)}, f32[40,256]{1,0:T(8,128)}, f32[64,256]{1,0:T(8,128)}, /*index=5*/f32[128,256]{1,0:T(8,128)}) custom-call(bf16[1024,256]{1,0:T(8,128)(2,1)S(1)} %get-tuple-element.18.refs_0_, bf16[2048,64]{1,0:T(8,128)(2,1)S(1)} %get-tuple-element.19.refs_1_, ...), custom_call_target="tpu_custom_call" | custom-call | tf_op jit(solution)/shard_map/pallas_call | solution.py:552

commit v5 on v4

--- a/solution.py
+++ b/solution.py
@@ -15,7 +15,7 @@
 CELLS = STRIP * WIDTH
 PIECES = ((32, 64), (96, 64), (160, 64), (0, 32), (224, 32))
 INNER, EDGES = (0, 1, 2), (3, 4)
-LAST_DOWN, LAST_UP = (0, 1), (2, 3, 4)
+LAST_DOWN, LAST_UP = (0, 2), (1, 3, 4)
 
 
 def nt(left, right):
@@ -34,7 +34,7 @@
     fl, og, fi, mi, ti, sw, fw, mw, tw,
     gf_o, gm_o, gt_o, kg_o, ml_o, tl_o,
     fl_v, g_v, fi_v, mi_v, ti_v, sw_v, fw_v, mw_v, tw_v,
-    big, wt, flt, lvl, tmp, fg, gath, top, macc,
+    big, flt, lvl, tmp, fg, gath, top, macc,
     term, crecv, csum, xrecv, zsend, zrecv, yown, yex,
     bterm, bxrecv, bz, bfin,
     in_sem, halo_s, halo_r, ring_s, edge_s, ring_r, last_r,
@@ -108,31 +108,10 @@
         big[pl.ds(first, rows), 2 * CH : 3 * CH] = before.astype(BF16)
 
     loads[0].wait()
-    pl.semaphore_wait(barrier, 7)
-
-    halo_down = remote(
-        g_v.at[pl.ds(CELLS, 64)], g_v.at[pl.ds(0, 64)], halo_s.at[0], halo_r.at[0], rows=down
-    )
-    halo_up = remote(
-        g_v.at[pl.ds(64, 64)], g_v.at[pl.ds(CELLS + 64, 64)], halo_s.at[0], halo_r.at[0], rows=up
-    )
-    halo_down.start()
-    halo_up.start()
-
 
     @pl.loop(0, 4)
     def _(t):
         widen(pl.multiple_of(64 + t * 256, 64), 256)
-
-    tell_y()
-    tell_z()
-    tell(seen_x, dict(dp_1=x_next), dict(dp_1=x_last))
-
-    loads[1].wait()
-
-    @pl.loop(0, 9)
-    def _(k):
-        wt[pl.ds(pl.multiple_of(k * CH, CH), CH), :] = sw_v[k].T
 
     def send_piece(p, away, stride, to_down):
         origin = lax.rem(y + NY - away, NY) if to_down else lax.rem(y + away, NY)
@@ -173,9 +152,13 @@
                     send_piece(p, 2, 2, to_down)
 
     def conv(rows):
-        total = nn(rows(128), wt[0:768, :])
-        total = total + nn(rows(64), wt[768:1536, :])
-        return total + nn(rows(0), wt[1536:2304, :])
+        total = None
+        for a in range(3):
+            value = rows(64 * (2 - a))
+            for b in range(3):
+                term_ab = nt(value[:, CH * b : CH * b + CH], sw_v[3 * a + b])
+                total = term_ab if total is None else total + term_ab
+        return total
 
     def pool(total, put):
         for j in range(2):
@@ -219,7 +202,27 @@
     for load in loads[3:]:
         load.start()
 
-    @pl.loop(0, 3)
+    loads[1].wait()
+    conv_inner(0)
+
+    pl.semaphore_wait(barrier, 7)
+
+    halo_down = remote(
+        g_v.at[pl.ds(CELLS, 64)], g_v.at[pl.ds(0, 64)], halo_s.at[0], halo_r.at[0], rows=down
+    )
+    halo_up = remote(
+        g_v.at[pl.ds(64, 64)], g_v.at[pl.ds(CELLS + 64, 64)], halo_s.at[0], halo_r.at[0], rows=up
+    )
+    halo_down.start()
+    halo_up.start()
+
+    tell_y()
+    tell_z()
+    tell(seen_x, dict(dp_1=x_next), dict(dp_1=x_last))
+
+    start_own(0)
+
+    @pl.loop(1, 3)
     def _(t):
         conv_inner(t)
         start_own(t)
@@ -346,12 +349,14 @@
                 z_copy(z_to).start()
 
     hear(seen_x)
-    forward(2, 0)
-
+    hear(seen_z)
+    tell_z()
     x_send(0)
 
     loads[3].wait()
     put_term(9, tn(fi_v[...], fg[...]))
+
+    forward(2, 0)
 
     forward(2, 1)
     forward(2, 2)
@@ -361,13 +366,14 @@
     macc[...] = jnp.zeros_like(macc)
     coarse(y)
 
+    hear(seen_z)
+    tell_z()
+
     x_send(1)
 
     hear(seen_y)
     edges_on()
     tell_y()
-    hear(seen_z)
-    tell_z()
 
     came(1, 3, True)
     came(1, 3, False)
@@ -386,8 +392,6 @@
         gf_o[rows, :] = nt(fg[rows, :], fw_v[...]).astype(BF16)
 
     hear(seen_y)
-    hear(seen_z)
-    tell_z()
     tell(seen_c, dict(dp_2=1 - c))
 
     came(3, 3, True)
@@ -515,7 +519,7 @@
     sizes = [
         ((CELLS, CH), BF16), ((CELLS + 128, CH), BF16), ((CELLS, CH), BF16), ((2048, 64), BF16),
         ((512, 128), BF16), ((9, CH, CH), BF16), ((CH, CH), BF16), ((64, CH), BF16), ((128, CH), BF16),
-        ((CELLS + 128, 3 * CH), BF16), ((9 * CH, CH), BF16), ((CH, CELLS), BF16),
+        ((CELLS + 128, 3 * CH), BF16), ((CH, CELLS), BF16),
         ((2, 128, 128), F32), ((2, 128, 128), F32), ((CELLS, CH), BF16),
         ((NY, CH, CH), BF16), ((64, CH), BF16), ((192, CH), F32),
         ((2, 2560, 128), BF16), ((2560, 128), BF16), ((2560, 128), BF16), ((NZ, NX - 1, 80, 128), BF16),

time: 46 us -> 45.3 us (0.985)
  Pallas kernels: 45.2 us -> 44.5 us
    pallas_call x1, Pallas kernels: 44 us -> 43.3 us  [body(): pl.pallas_call(kernel, out_shape=[pltpu.VMEM(*shape) for shape in shapes]...]
where the time goes in v5:
time: 45.3 us; the launch traced here: 45.1 us
  Pallas kernels  44.5 us (98%)
  between operations  0.64 us (1%)
    pallas_call x1, Pallas kernels, body(): pl.pallas_call(kernel, out_shape=[pltpu.VMEM(*shape) for shape in shapes]...  43.3 us
    pallas_call x1, Pallas kernels, body(): pl.pallas_call(store, out_shape=[pltpu.HBM(*shape) for shape in shapes],...  1.13 us

profile of v5, /device:TPU:1, one launch (start us, length us, event | category | flops | bytes accessed | tf_op | source)
XLA Modules:
  0.0 45.1 jit_solution(13877783859681582593)
XLA Ops:
  0.6 43.3 %shard_map.136 = (bf16[1024,256]{1,0:T(8,128)(2,1)S(1)}, bf16[2048,64]{1,0:T(8,128)(2,1)S(1)}, bf16[512,128]{1,0:T(8,128)(2,1)S(1)}, f32[40,256]{1,0:T(8,128)S(1...) custom-call(bf16[1024,256]{1,0:T(8,128)(2,1)} %bitcast.10, bf16[1024,256]{1,0:T(8,128)(2,1)} %bitcast.11, ...), custom_call_target="tpu_custom_call" | custom-call | tf_op jit(solution)/shard_map/pallas_call | solution.py:541
  44.0 1.1 %shard_map.137 = (bf16[1024,256]{1,0:T(8,128)(2,1)}, bf16[2048,64]{1,0:T(8,128)(2,1)}, bf16[512,128]{1,0:T(8,128)(2,1)}, f32[40,256]{1,0:T(8,128)}, f32[64,256]{1,0:T(8,128)}, /*index=5*/f32[128,256]{1,0:T(8,128)}) custom-call(bf16[1024,256]{1,0:T(8,128)(2,1)S(1)} %get-tuple-element.18.refs_0_, bf16[2048,64]{1,0:T(8,128)(2,1)S(1)} %get-tuple-element.19.refs_1_, ...), custom_call_target="tpu_custom_call" | custom-call | tf_op jit(solution)/shard_map/pallas_call | solution.py:556

commit v6 on v5

--- a/solution.py
+++ b/solution.py
@@ -13,9 +13,9 @@
 NZ, NX, NC, NY = 8, 4, 2, 8
 STRIP, WIDTH, CH = 16, 64, 256
 CELLS = STRIP * WIDTH
-PIECES = ((32, 64), (96, 64), (160, 64), (0, 32), (224, 32))
-INNER, EDGES = (0, 1, 2), (3, 4)
-LAST_DOWN, LAST_UP = (0, 2), (1, 3, 4)
+PIECES = ((64, 64), (128, 64), (192, 64), (0, 64))
+INNER, EDGES = (0, 1, 2), (3,)
+LAST_DOWN, LAST_UP = (0, 2), (1, 3)
 
 
 def nt(left, right):
@@ -116,7 +116,7 @@
     def send_piece(p, away, stride, to_down):
         origin = lax.rem(y + NY - away, NY) if to_down else lax.rem(y + away, NY)
         target = lax.rem(y + stride, NY) if to_down else lax.rem(y + NY - stride, NY)
-        first, count = PIECES[p] if isinstance(p, int) else (pl.multiple_of(32 + 64 * p, 32), 64)
+        first, count = PIECES[p] if isinstance(p, int) else (pl.multiple_of(64 + 64 * p, 64), 64)
         block = gath.at[origin, pl.ds(first, count)]
         h = away + stride
         group = 3 if isinstance(p, int) and p in EDGES else p
@@ -174,7 +174,7 @@
 
     def conv_inner(t):
         first = pl.multiple_of(128 + 256 * t, 128)
-        out = pl.multiple_of(32 + 64 * t, 32)
+        out = pl.multiple_of(64 + 64 * t, 64)
         total = conv(lambda shift: big[pl.ds(first + shift, 256), :])
         fg[pl.ds(first, 256), :] = total.astype(BF16)
 
@@ -194,8 +194,7 @@
         fg[low:CELLS, :] = total[128:256].astype(BF16)
 
         def put(j, pooled):
-            gath[y, 0:32, 128 * j : 128 * j + 128] = pooled[0:32]
-            gath[y, 224:256, 128 * j : 128 * j + 128] = pooled[32:64]
+            gath[y, 0:64, 128 * j : 128 * j + 128] = pooled
 
         pool(total, put)
 
@@ -256,6 +255,8 @@
     def _(k):
         tap(k)
 
+    forward(1, 0)
+
     wait_bytes(g_v.at[pl.ds(0, 128)], halo_r.at[0])
 
     @pl.when(y == 0)
@@ -270,21 +271,22 @@
     widen(CELLS + 64, 64)
 
     conv_edges()
+    forward(1, 1)
+    forward(1, 2)
     hear(seen_y)
     edges_from_home()
     tell_y()
 
     @pl.loop(0, 3)
-    def _(p):
-        forward(1, p)
-        tap(p)
+    def _(k):
+        tap(k)
 
     @pl.loop(6, 9)
     def _(k):
         tap(k)
 
     def coarse(s):
-        mid = gath[s]
+        mid = jnp.concatenate([gath[s, 0:32], gath[s, 64:256], gath[s, 32:64]])
         cells = pl.ds(pl.multiple_of(s * CH, CH), CH)
         gm_o[cells, :] = nt(mid, mw_v[...]).astype(BF16)
         macc[0:64, :] += tn(mi_v[cells, :], mid)
@@ -351,12 +353,12 @@
     hear(seen_x)
     hear(seen_z)
     tell_z()
+    forward(2, 0)
+
     x_send(0)
 
     loads[3].wait()
     put_term(9, tn(fi_v[...], fg[...]))
-
-    forward(2, 0)
 
     forward(2, 1)
     forward(2, 2)

time: 45.3 us -> 44.4 us (0.980)
  Pallas kernels: 44.5 us -> 43.6 us
    pallas_call x1, Pallas kernels: 43.3 us -> 42.4 us  [body(): pl.pallas_call(kernel, out_shape=[pltpu.VMEM(*shape) for shape in shapes]...]
where the time goes in v6:
time: 44.4 us; the launch traced here: 44.2 us
  Pallas kernels  43.6 us (98%)
  between operations  0.64 us (1%)
    pallas_call x1, Pallas kernels, body(): pl.pallas_call(kernel, out_shape=[pltpu.VMEM(*shape) for shape in shapes]...  42.4 us
    pallas_call x1, Pallas kernels, body(): pl.pallas_call(store, out_shape=[pltpu.HBM(*shape) for shape in shapes],...  1.13 us

profile of v6, /device:TPU:1, one launch (start us, length us, event | category | flops | bytes accessed | tf_op | source)
XLA Modules:
  0.0 44.2 jit_solution(12767031735670037147)
XLA Ops:
  0.6 42.4 %shard_map.136 = (bf16[1024,256]{1,0:T(8,128)(2,1)S(1)}, bf16[2048,64]{1,0:T(8,128)(2,1)S(1)}, bf16[512,128]{1,0:T(8,128)(2,1)S(1)}, f32[40,256]{1,0:T(8,128)S(1...) custom-call(bf16[1024,256]{1,0:T(8,128)(2,1)} %bitcast.10, bf16[1024,256]{1,0:T(8,128)(2,1)} %bitcast.11, ...), custom_call_target="tpu_custom_call" | custom-call | tf_op jit(solution)/shard_map/pallas_call | solution.py:543
  43.1 1.1 %shard_map.137 = (bf16[1024,256]{1,0:T(8,128)(2,1)}, bf16[2048,64]{1,0:T(8,128)(2,1)}, bf16[512,128]{1,0:T(8,128)(2,1)}, f32[40,256]{1,0:T(8,128)}, f32[64,256]{1,0:T(8,128)}, /*index=5*/f32[128,256]{1,0:T(8,128)}) custom-call(bf16[1024,256]{1,0:T(8,128)(2,1)S(1)} %get-tuple-element.18.refs_0_, bf16[2048,64]{1,0:T(8,128)(2,1)S(1)} %get-tuple-element.19.refs_1_, ...), custom_call_target="tpu_custom_call" | custom-call | tf_op jit(solution)/shard_map/pallas_call | solution.py:558

commit v7 on v6

--- a/solution.py
+++ b/solution.py
@@ -15,6 +15,7 @@
 CELLS = STRIP * WIDTH
 PIECES = ((64, 64), (128, 64), (192, 64), (0, 64))
 INNER, EDGES = (0, 1, 2), (3,)
+X_FAR, FAR = (2, 1, 3), (4, 3, 5, 2, 6, 1, 7)
 LAST_DOWN, LAST_UP = (0, 2), (1, 3)
 
 
@@ -328,7 +329,7 @@
 
         @pl.loop(4 * batch, 4 * batch + 4)
         def _(s):
-            for d in range(1, NX):
+            for d in X_FAR:
                 x_copy(s, d).start()
 
     def z_copy(z_to):
@@ -353,9 +354,9 @@
     hear(seen_x)
     hear(seen_z)
     tell_z()
+    x_send(0)
+
     forward(2, 0)
-
-    x_send(0)
 
     loads[3].wait()
     put_term(9, tn(fi_v[...], fg[...]))
@@ -411,7 +412,7 @@
     coarse(lax.rem(y + 4, NY))
     hear(seen_c, 1)
 
-    others = [(d, e) for d in range(NX) for e in range(NC) if d or e]
+    others = [(d, e) for d in X_FAR for e in (1, 0)] + [(0, 1)]
     for i in range(NX):
         for j in range(NC):
             bterm[NC * i + j] = macc[48 * i : 48 * i + 48, 128 * j : 128 * j + 128].astype(BF16)
@@ -437,7 +438,7 @@
     def bz_copy(d):
         return remote(bz.at[z], bz.at[z], bz_s.at[0], bz_r.at[0], dp_0=lax.rem(z + d, NZ))
 
-    for d in range(1, NZ):
+    for d in FAR:
         bz_copy(d).start()
 
     wait_bytes(zrecv, z_r.at[0])
@@ -455,10 +456,10 @@
             rows=lax.rem(y + d, NY), dp_2=c_to,
         )
 
-    for d in range(NY):
-        for e in range(NC):
-            if d or e:
-                y_copy(d, e).start()
+    for d in FAR:
+        for e in (1, 0):
+            y_copy(d, e).start()
+    y_copy(0, 1).start()
 
     wait_bytes(bz.at[pl.ds(0, NZ - 1)], bz_r.at[0])
     total = bz[0].astype(F32)

time: 44.4 us -> 43.7 us (0.984)
  Pallas kernels: 43.6 us -> 42.9 us
    pallas_call x1, Pallas kernels: 42.4 us -> 41.7 us  [body(): pl.pallas_call(kernel, out_shape=[pltpu.VMEM(*shape) for shape in shapes]...]
where the time goes in v7:
time: 43.7 us; the launch traced here: 43.5 us
  Pallas kernels  42.9 us (98%)
  between operations  0.64 us (1%)
    pallas_call x1, Pallas kernels, body(): pl.pallas_call(kernel, out_shape=[pltpu.VMEM(*shape) for shape in shapes]...  41.7 us
    pallas_call x1, Pallas kernels, body(): pl.pallas_call(store, out_shape=[pltpu.HBM(*shape) for shape in shapes],...  1.13 us

profile of v7, /device:TPU:1, one launch (start us, length us, event | category | flops | bytes accessed | tf_op | source)
XLA Modules:
  0.0 43.5 jit_solution(11677754766379255673)
XLA Ops:
  0.6 41.7 %shard_map.136 = (bf16[1024,256]{1,0:T(8,128)(2,1)S(1)}, bf16[2048,64]{1,0:T(8,128)(2,1)S(1)}, bf16[512,128]{1,0:T(8,128)(2,1)S(1)}, f32[40,256]{1,0:T(8,128)S(1...) custom-call(bf16[1024,256]{1,0:T(8,128)(2,1)} %bitcast.10, bf16[1024,256]{1,0:T(8,128)(2,1)} %bitcast.11, ...), custom_call_target="tpu_custom_call" | custom-call | tf_op jit(solution)/shard_map/pallas_call | solution.py:544
  42.4 1.1 %shard_map.137 = (bf16[1024,256]{1,0:T(8,128)(2,1)}, bf16[2048,64]{1,0:T(8,128)(2,1)}, bf16[512,128]{1,0:T(8,128)(2,1)}, f32[40,256]{1,0:T(8,128)}, f32[64,256]{1,0:T(8,128)}, /*index=5*/f32[128,256]{1,0:T(8,128)}) custom-call(bf16[1024,256]{1,0:T(8,128)(2,1)S(1)} %get-tuple-element.18.refs_0_, bf16[2048,64]{1,0:T(8,128)(2,1)S(1)} %get-tuple-element.19.refs_1_, ...), custom_call_target="tpu_custom_call" | custom-call | tf_op jit(solution)/shard_map/pallas_call | solution.py:559

commit v8 on v7

--- a/solution.py
+++ b/solution.py
@@ -139,7 +139,7 @@
                 send_piece(p, h, 1, to_down)
 
     def edges_from_home():
-        for stride in (1, 2):
+        for stride in (2, 1):
             for p in EDGES:
                 send_piece(p, 0, stride, True)
                 send_piece(p, 0, stride, False)
@@ -148,9 +148,9 @@
         for to_down in (True, False):
             came(2, 3, to_down)
             for p in EDGES:
-                send_piece(p, 2, 1, to_down)
                 if p in (LAST_DOWN if to_down else LAST_UP):
                     send_piece(p, 2, 2, to_down)
+                send_piece(p, 2, 1, to_down)
 
     def conv(rows):
         total = None
@@ -213,14 +213,13 @@
     halo_up = remote(
         g_v.at[pl.ds(64, 64)], g_v.at[pl.ds(CELLS + 64, 64)], halo_s.at[0], halo_r.at[0], rows=up
     )
+    start_own(0)
     halo_down.start()
     halo_up.start()
 
     tell_y()
     tell_z()
     tell(seen_x, dict(dp_1=x_next), dict(dp_1=x_last))
-
-    start_own(0)
 
     @pl.loop(1, 3)
     def _(t):
@@ -354,12 +353,12 @@
     hear(seen_x)
     hear(seen_z)
     tell_z()
-    x_send(0)
-
-    forward(2, 0)
-
     loads[3].wait()
     put_term(9, tn(fi_v[...], fg[...]))
+
+    forward(2, 0)
+
+    x_send(0)
 
     forward(2, 1)
     forward(2, 2)
@@ -372,11 +371,11 @@
     hear(seen_z)
     tell_z()
 
-    x_send(1)
-
     hear(seen_y)
     edges_on()
     tell_y()
+
+    x_send(1)
 
     came(1, 3, True)
     came(1, 3, False)

time: 43.7 us -> 44.4 us (1.016)
  Pallas kernels: 42.9 us -> 43.6 us
    pallas_call x1, Pallas kernels: 41.7 us -> 42.5 us  [body(): pl.pallas_call(kernel, out_shape=[pltpu.VMEM(*shape) for shape in shapes]...]
where the time goes in v8:
time: 44.4 us; the launch traced here: 44.3 us
  Pallas kernels  43.6 us (98%)
  between operations  0.64 us (1%)
    pallas_call x1, Pallas kernels, body(): pl.pallas_call(kernel, out_shape=[pltpu.VMEM(*shape) for shape in shapes]...  42.5 us
    pallas_call x1, Pallas kernels, body(): pl.pallas_call(store, out_shape=[pltpu.HBM(*shape) for shape in shapes],...  1.13 us

profile of v8, /device:TPU:1, one launch (start us, length us, event | category | flops | bytes accessed | tf_op | source)
XLA Modules:
  0.0 44.3 jit_solution(10137905121218956208)
XLA Ops:
  0.6 42.5 %shard_map.136 = (bf16[1024,256]{1,0:T(8,128)(2,1)S(1)}, bf16[2048,64]{1,0:T(8,128)(2,1)S(1)}, bf16[512,128]{1,0:T(8,128)(2,1)S(1)}, f32[40,256]{1,0:T(8,128)S(1...) custom-call(bf16[1024,256]{1,0:T(8,128)(2,1)} %bitcast.10, bf16[1024,256]{1,0:T(8,128)(2,1)} %bitcast.11, ...), custom_call_target="tpu_custom_call" | custom-call | tf_op jit(solution)/shard_map/pallas_call | solution.py:543
  43.1 1.1 %shard_map.137 = (bf16[1024,256]{1,0:T(8,128)(2,1)}, bf16[2048,64]{1,0:T(8,128)(2,1)}, bf16[512,128]{1,0:T(8,128)(2,1)}, f32[40,256]{1,0:T(8,128)}, f32[64,256]{1,0:T(8,128)}, /*index=5*/f32[128,256]{1,0:T(8,128)}) custom-call(bf16[1024,256]{1,0:T(8,128)(2,1)S(1)} %get-tuple-element.18.refs_0_, bf16[2048,64]{1,0:T(8,128)(2,1)S(1)} %get-tuple-element.19.refs_1_, ...), custom_call_target="tpu_custom_call" | custom-call | tf_op jit(solution)/shard_map/pallas_call | solution.py:558

commit v9 on v7

--- a/solution.py
+++ b/solution.py
@@ -286,10 +286,9 @@
     def _(k):
         tap(k)
 
-    def coarse(s):
+    def coarse_sums(s):
         mid = jnp.concatenate([gath[s, 0:32], gath[s, 64:256], gath[s, 32:64]])
         cells = pl.ds(pl.multiple_of(s * CH, CH), CH)
-        gm_o[cells, :] = nt(mid, mw_v[...]).astype(BF16)
         macc[0:64, :] += tn(mi_v[cells, :], mid)
         wide = mid.astype(F32)
         for j in range(2):
@@ -303,8 +302,15 @@
             ).astype(BF16)
         small = top[...]
         cells = pl.ds(pl.multiple_of(s * 64, 64), 64)
-        gt_o[cells, :] = nt(small, tw_v[...]).astype(BF16)
         macc[64:192, :] += tn(ti_v[cells, :], small)
+        return mid, small
+
+    def coarse_maps(s, mid, small):
+        gm_o[pl.ds(pl.multiple_of(s * CH, CH), CH), :] = nt(mid, mw_v[...]).astype(BF16)
+        gt_o[pl.ds(pl.multiple_of(s * 64, 64), 64), :] = nt(small, tw_v[...]).astype(BF16)
+
+    def coarse(s):
+        coarse_maps(s, *coarse_sums(s))
 
     def core_sum(k):
         rows = pl.ds(pl.multiple_of(k * CH, CH), CH)
@@ -409,7 +415,8 @@
 
     wait_bytes(gath.at[0], last_r.at[0])
 
-    coarse(lax.rem(y + 4, NY))
+    far = lax.rem(y + 4, NY)
+    far_maps = coarse_sums(far)
     hear(seen_c, 1)
 
     others = [(d, e) for d in X_FAR for e in (1, 0)] + [(0, 1)]
@@ -426,6 +433,8 @@
 
     for d, e in others:
         bx_copy(d, e).start()
+
+    coarse_maps(far, *far_maps)
 
     x_reduce(1)
 

time: 43.7 us -> 43.6 us (level)
  no operation moved by 1% of the time
where the time goes in v9:
time: 43.6 us; the launch traced here: 43.5 us
  Pallas kernels  42.8 us (98%)
  between operations  0.64 us (1%)
    pallas_call x1, Pallas kernels, body(): pl.pallas_call(kernel, out_shape=[pltpu.VMEM(*shape) for shape in shapes]...  41.7 us
    pallas_call x1, Pallas kernels, body(): pl.pallas_call(store, out_shape=[pltpu.HBM(*shape) for shape in shapes],...  1.13 us

profile of v9, /device:TPU:1, one launch (start us, length us, event | category | flops | bytes accessed | tf_op | source)
XLA Modules:
  0.0 43.5 jit_solution(2740015773336031949)
XLA Ops:
  0.6 41.7 %shard_map.136 = (bf16[1024,256]{1,0:T(8,128)(2,1)S(1)}, bf16[2048,64]{1,0:T(8,128)(2,1)S(1)}, bf16[512,128]{1,0:T(8,128)(2,1)S(1)}, f32[40,256]{1,0:T(8,128)S(1...) custom-call(bf16[1024,256]{1,0:T(8,128)(2,1)} %bitcast.10, bf16[1024,256]{1,0:T(8,128)(2,1)} %bitcast.11, ...), custom_call_target="tpu_custom_call" | custom-call | tf_op jit(solution)/shard_map/pallas_call | solution.py:553
  42.4 1.1 %shard_map.137 = (bf16[1024,256]{1,0:T(8,128)(2,1)}, bf16[2048,64]{1,0:T(8,128)(2,1)}, bf16[512,128]{1,0:T(8,128)(2,1)}, f32[40,256]{1,0:T(8,128)}, f32[64,256]{1,0:T(8,128)}, /*index=5*/f32[128,256]{1,0:T(8,128)}) custom-call(bf16[1024,256]{1,0:T(8,128)(2,1)S(1)} %get-tuple-element.18.refs_0_, bf16[2048,64]{1,0:T(8,128)(2,1)S(1)} %get-tuple-element.19.refs_1_, ...), custom_call_target="tpu_custom_call" | custom-call | tf_op jit(solution)/shard_map/pallas_call | solution.py:568
